TPU v7x, 1024 devices: a whole 8x8x8 slice. The times are simulated.
1024 devices in a mesh: gx: 16 (over x, core), gy: 8 (over z), gz: 8 (over y).
Axes of the slice: x: 8, y: 8, z: 8, core: 2. Of those that a mesh axis runs over, the one named last changes fastest.
Arguments:
- field: float32 [256, 128, 1024], P('gx', 'gz', 'gy'), may hold values from -6 to 6
Outputs:
- coefficients: float32 [256, 128, 1024], P('gx', 'gz', 'gy')
All inputs are finite; a program needn't handle non-finite values.
Results may differ from a plain program's by a relative error of at most 0.00002.
Values sent between devices are 32-bit elements; how exact they have to be, the bound alone decides.
No kernel may reach another device: no remote copies, remote signals or barrier semaphores. Data moves between devices by JAX's collectives and lax.ppermute only.
A program may use at most 32 MiB of HBM per device.

v0:
```python
import jax
import jax.numpy as jnp
from jax import lax
from jax.sharding import PartitionSpec as P

ALPHA = -1.586134342
BETA = -0.05298011854
GAMMA = 0.8829110762
DELTA = 0.4435068522
ZETA = 1.149604398


def padded_2(block, sides, width):
    for axis, dim in sides:
        count = lax.axis_size(axis)
        forward = [(i, i + 1) for i in range(count - 1)]
        backward = [(target, source) for source, target in forward]
        low = lax.ppermute(
            lax.slice_in_dim(block, block.shape[dim] - width, None, axis=dim), axis, forward
        )
        high = lax.ppermute(lax.slice_in_dim(block, 0, width, axis=dim), axis, backward)
        block = jnp.concatenate([low, block, high], axis=dim)
    return block


def piece(array, start, stop, dim):
    return lax.slice_in_dim(array, start, stop, axis=dim)


def lift_padded(padded, dim):
    total = padded.shape[dim]
    half = total // 2
    shape = padded.shape[:dim] + (half, 2) + padded.shape[dim + 1 :]
    pairs = padded.reshape(shape)
    even = lax.index_in_dim(pairs, 0, dim + 1, keepdims=False)
    odd = lax.index_in_dim(pairs, 1, dim + 1, keepdims=False)
    odd_one = piece(odd, 0, half - 1, dim) + ALPHA * (
        piece(even, 0, half - 1, dim) + piece(even, 1, half, dim)
    )
    even_two = piece(even, 1, half - 1, dim) + BETA * (
        piece(odd_one, 0, half - 2, dim) + piece(odd_one, 1, half - 1, dim)
    )
    odd_three = piece(odd_one, 1, half - 2, dim) + GAMMA * (
        piece(even_two, 0, half - 3, dim) + piece(even_two, 1, half - 2, dim)
    )
    even_four = piece(even_two, 1, half - 3, dim) + DELTA * (
        piece(odd_three, 0, half - 4, dim) + piece(odd_three, 1, half - 3, dim)
    )
    lowpass = even_four * ZETA
    highpass = piece(odd_three, 1, half - 3, dim) / ZETA
    joined = jnp.stack([lowpass, highpass], axis=dim + 1)
    out_shape = padded.shape[:dim] + (total - 8,) + padded.shape[dim + 1 :]
    return joined.reshape(out_shape)


def mirror(extended, dim, first, last, width):
    length = extended.shape[dim] - 2 * width
    left = jnp.where(
        first,
        lax.rev(piece(extended, width + 1, 2 * width + 1, dim), (dim,)),
        piece(extended, 0, width, dim),
    )
    right = jnp.where(
        last,
        lax.rev(piece(extended, length - 1, length + width - 1, dim), (dim,)),
        piece(extended, length + width, length + 2 * width, dim),
    )
    return jnp.concatenate([left, piece(extended, width, length + width, dim), right], axis=dim)


def at_ends(where, count):
    return (where == 0, where == count - 1)


def on_device(field):
    first_x, last_x = at_ends(lax.axis_index("gx"), lax.axis_size("gx"))
    first_y, last_y = at_ends(lax.axis_index("gy"), lax.axis_size("gy"))
    first_z, last_z = at_ends(lax.axis_index("gz"), lax.axis_size("gz"))
    extended = padded_2(field, (("gx", 0),), 4)
    level_one = lift_padded(mirror(extended, 0, first_x, last_x, 4), 0)
    extended = padded_2(level_one, (("gz", 1),), 4)
    level_one = lift_padded(mirror(extended, 1, first_z, last_z, 4), 1)
    extended = padded_2(level_one, (("gy", 2),), 4)
    level_one = lift_padded(mirror(extended, 2, first_y, last_y, 4), 2)
    coarse = level_one[::2, ::2, ::2]
    extended = padded_2(coarse, (("gx", 0),), 4)
    coarse = lift_padded(mirror(extended, 0, first_x, last_x, 4), 0)
    extended = padded_2(coarse, (("gz", 1),), 4)
    coarse = lift_padded(mirror(extended, 1, first_z, last_z, 4), 1)
    extended = padded_2(coarse, (("gy", 2),), 4)
    coarse = lift_padded(mirror(extended, 2, first_y, last_y, 4), 2)
    return level_one.at[::2, ::2, ::2].set(coarse)


def solution(mesh):
    placed = (P("gx", "gz", "gy"),)
    return jax.shard_map(
        on_device, mesh=mesh, in_specs=placed, out_specs=P("gx", "gz", "gy"), check_vma=False
    )
```

profile of v0, /device:TPU:39, one launch (start us, length us, event | category | flops | bytes accessed | tf_op | source)
XLA Modules:
  0.0 111.6 jit_solution(17922987898087644049)
XLA Ops:
  0.0 0.8 fusion.68
  0.8 4.9 %collective-permute-start = (f32[4,16,128]{2,1,0:T(8,128)S(1)}, f32[4,16,128]{2,1,0:T(8,128)S(1)}, u32[]{:S(2)}, u32[]{:S(2)}) collective-permute-start(f32[4,16,128]{2,1,0:T(8,128)S(1)} %get-tuple-element.32), channel_id=1, source_target_pairs={{0,64},{64,128},{128,192},{192,256},{256,320},{320,384},{384,448},... | collective-permute-start | bytes 98312 | tf_op jit(solution)/shard_map/ppermute | solution.py:18
  5.7 1.9 %collective-permute-start.1 = (f32[4,16,128]{2,1,0:T(8,128)S(1)}, f32[4,16,128]{2,1,0:T(8,128)S(1)}, u32[]{:S(2)}, u32[]{:S(2)}) collective-permute-start(f32[4,16,128]{2,1,0:T(8,128)S(1)} %get-tuple-element.33), channel_id=1, source_target_pairs={{64,0},{128,64},{192,128},{256,192},{320,256},{384,320},{448,384},... | collective-permute-start | bytes 98312 | tf_op jit(solution)/shard_map/ppermute | solution.py:21
  7.7 4.5 %collective-permute-done.1 = f32[4,16,128]{2,1,0:T(8,128)S(1)} collective-permute-done((f32[4,16,128]{2,1,0:T(8,128)S(1)}, f32[4,16,128]{2,1,0:T(8,128)S(1)}, u32[]{:S(2)}, u32[]{:S(2)}) %collective-permute-start.1) | collective-permute-done | bytes 32800 | tf_op jit(solution)/shard_map/ppermute | solution.py:21
  12.2 0.9 pad_maximum_fusion.3
  13.2 0.2 fusion.29
  13.4 0.1 fusion.33
  13.6 0.1 fusion.37
  13.7 0.2 fusion.44
  13.8 0.1 pad_maximum_fusion.5
  14.0 3.3 %collective-permute-start.2 = (f32[16,4,128]{2,0,1:T(8,128)S(1)}, f32[16,4,128]{2,0,1:T(8,128)S(1)}, u32[]{:S(2)}, u32[]{:S(2)}) collective-permute-start(f32[16,4,128]{2,0,1:T(8,128)S(1)} %get-tuple-element.29), channel_id=1, source_target_pairs={{0,1},{1,2},{2,3},{3,4},{4,5},{5,6},{6,7},{8,9},{9,10},{10,11},{11... | collective-permute-start | bytes 98312 | tf_op jit(solution)/shard_map/ppermute | solution.py:18
  17.3 2.0 %collective-permute-start.3 = (f32[16,4,128]{2,0,1:T(8,128)S(1)}, f32[16,4,128]{2,0,1:T(8,128)S(1)}, u32[]{:S(2)}, u32[]{:S(2)}) collective-permute-start(f32[16,4,128]{2,0,1:T(8,128)S(1)} %get-tuple-element.27), channel_id=1, source_target_pairs={{1,0},{2,1},{3,2},{4,3},{5,4},{6,5},{7,6},{9,8},{10,9},{11,10},{12... | collective-permute-start | bytes 98312 | tf_op jit(solution)/shard_map/ppermute | solution.py:21
  19.3 3.8 %collective-permute-done.3 = f32[16,4,128]{2,0,1:T(8,128)S(1)} collective-permute-done((f32[16,4,128]{2,0,1:T(8,128)S(1)}, f32[16,4,128]{2,0,1:T(8,128)S(1)}, u32[]{:S(2)}, u32[]{:S(2)}) %collective-permute-start.3) | collective-permute-done | bytes 32800 | tf_op jit(solution)/shard_map/ppermute | solution.py:21
  23.3 0.2 fusion.66
  23.5 4.9 %collective-permute-start.4 = (f32[16,16,4]{2,0,1:T(8,128)S(1)}, f32[16,16,4]{2,0,1:T(8,128)S(1)}, u32[]{:S(2)}, u32[]{:S(2)}) collective-permute-start(f32[16,16,4]{2,0,1:T(8,128)S(1)} %get-tuple-element.22), channel_id=1, source_target_pairs={{0,8},{8,16},{16,24},{24,32},{32,40},{40,48},{48,56},{1,9},{9,17},... | collective-permute-start | bytes 12296 | tf_op jit(solution)/shard_map/ppermute | solution.py:18
  28.5 0.1 rev.40
  28.5 1.3 %collective-permute-start.5 = (f32[16,16,4]{2,0,1:T(8,128)S(1)}, f32[16,16,4]{2,0,1:T(8,128)S(1)}, u32[]{:S(2)}, u32[]{:S(2)}) collective-permute-start(f32[16,16,4]{2,0,1:T(8,128)S(1)} %get-tuple-element.23), channel_id=1, source_target_pairs={{8,0},{16,8},{24,16},{32,24},{40,32},{48,40},{56,48},{9,1},{17,9},... | collective-permute-start | bytes 12296 | tf_op jit(solution)/shard_map/ppermute | solution.py:21
  29.8 0.1 rev.41
  29.9 0.4 collective-permute-done.4
  30.4 5.4 %collective-permute-done.5 = f32[16,16,4]{2,0,1:T(8,128)S(1)} collective-permute-done((f32[16,16,4]{2,0,1:T(8,128)S(1)}, f32[16,16,4]{2,0,1:T(8,128)S(1)}, u32[]{:S(2)}, u32[]{:S(2)}) %collective-permute-start.5) | collective-permute-done | bytes 4128 | tf_op jit(solution)/shard_map/ppermute | solution.py:21
  35.8 0.2 pad_maximum_fusion.1
  36.0 0.6 copy.63
  36.6 0.1 slice_bitcast_fusion
  36.7 0.1 fusion.1
  36.8 0.1 fusion.3
  36.9 0.1 fusion.5
  36.9 0.1 fusion.9
  37.1 0.1 pad_maximum_fusion
  37.1 0.1 copy.67
  37.3 0.0 copy-start.2
  37.3 5.3 %slice.409 = f32[8,8,64]{1,0,2:T(8,128)S(1)} slice(f32[16,16,128]{1,0,2:T(8,128)S(1)} %bitcast.59), slice={[0:16:2], [0:16:2], [0:128:2]} | slice | bytes 32768 | tf_op jit(solution)/shard_map/slice | solution.py:85
  42.6 0.1 fusion.64
  42.7 4.2 %collective-permute-start.6 = (f32[4,8,64]{1,0,2:T(4,128)S(1)}, f32[4,8,64]{1,0,2:T(4,128)S(1)}, u32[]{:S(2)}, u32[]{:S(2)}) collective-permute-start(f32[4,8,64]{1,0,2:T(4,128)S(1)} %get-tuple-element.11), channel_id=1, source_target_pairs={{0,64},{64,128},{128,192},{192,256},{256,320},{320,384},{384,448},... | collective-permute-start | bytes 24584 | tf_op jit(solution)/shard_map/ppermute | solution.py:18
  47.0 0.1 broadcast_in_dim.10
  47.0 0.1 broadcast_in_dim.9
  47.1 0.1 fusion.25
  47.2 0.1 copy.69
  47.3 0.2 rev.42
  47.5 0.0 copy-start.1
  47.5 1.9 %collective-permute-start.7 = (f32[4,8,64]{1,0,2:T(4,128)S(1)}, f32[4,8,64]{1,0,2:T(4,128)S(1)}, u32[]{:S(2)}, u32[]{:S(2)}) collective-permute-start(f32[4,8,64]{1,0,2:T(4,128)S(1)} %get-tuple-element.12), channel_id=1, source_target_pairs={{64,0},{128,64},{192,128},{256,192},{320,256},{384,320},{448,384},... | collective-permute-start | bytes 24584 | tf_op jit(solution)/shard_map/ppermute | solution.py:21
  49.4 0.2 rev.43
  49.6 0.1 copy.68
  49.7 5.3 %collective-permute-done.7 = f32[4,8,64]{1,0,2:T(4,128)S(1)} collective-permute-done((f32[4,8,64]{1,0,2:T(4,128)S(1)}, f32[4,8,64]{1,0,2:T(4,128)S(1)}, u32[]{:S(2)}, u32[]{:S(2)}) %collective-permute-start.7) | collective-permute-done | bytes 8224 | tf_op jit(solution)/shard_map/ppermute | solution.py:21
  55.0 0.1 copy.70
  55.2 4.9 %collective-permute-start.8 = (f32[8,4,64]{2,0,1:T(8,128)S(1)}, f32[8,4,64]{2,0,1:T(8,128)S(1)}, u32[]{:S(2)}, u32[]{:S(2)}) collective-permute-start(f32[8,4,64]{2,0,1:T(8,128)S(1)} %get-tuple-element.47), channel_id=1, source_target_pairs={{0,1},{1,2},{2,3},{3,4},{4,5},{5,6},{6,7},{8,9},{9,10},{10,11},{11... | collective-permute-start | bytes 24584 | tf_op jit(solution)/shard_map/ppermute | solution.py:18
  60.1 0.1 fusion.23
  60.2 1.9 %collective-permute-start.9 = (f32[8,4,64]{2,0,1:T(8,128)S(1)}, f32[8,4,64]{2,0,1:T(8,128)S(1)}, u32[]{:S(2)}, u32[]{:S(2)}) collective-permute-start(f32[8,4,64]{2,0,1:T(8,128)S(1)} %get-tuple-element.45), channel_id=1, source_target_pairs={{1,0},{2,1},{3,2},{4,3},{5,4},{6,5},{7,6},{9,8},{10,9},{11,10},{12... | collective-permute-start | bytes 24584 | tf_op jit(solution)/shard_map/ppermute | solution.py:21
  62.2 2.5 %collective-permute-done.9 = f32[8,4,64]{2,0,1:T(8,128)S(1)} collective-permute-done((f32[8,4,64]{2,0,1:T(8,128)S(1)}, f32[8,4,64]{2,0,1:T(8,128)S(1)}, u32[]{:S(2)}, u32[]{:S(2)}) %collective-permute-start.9) | collective-permute-done | bytes 8224 | tf_op jit(solution)/shard_map/ppermute | solution.py:21
  64.8 0.1 fusion.69
  64.9 4.9 %collective-permute-start.10 = (f32[8,8,4]{2,0,1:T(8,128)S(1)}, f32[8,8,4]{2,0,1:T(8,128)S(1)}, u32[]{:S(2)}, u32[]{:S(2)}) collective-permute-start(f32[8,8,4]{2,0,1:T(8,128)S(1)} %get-tuple-element.40), channel_id=1, source_target_pairs={{0,8},{8,16},{16,24},{24,32},{32,40},{40,48},{48,56},{1,9},{9,17},... | collective-permute-start | bytes 3080 | tf_op jit(solution)/shard_map/ppermute | solution.py:18
  69.8 0.1 reshape.95
  69.9 8.5 %copy.66 = f32[16,16,64,2]{3,2,1,0:T(8,128)} copy(f32[16,16,64,2]{1,0,2,3:T(8,128)S(1)} %pad_maximum_fusion) | data formatting | bytes 262144 | tf_op jit(solution)/shard_map/stack | solution.py:51
  78.4 6.9 %reshape.73 = f32[32768]{0:T(1024)S(1)} reshape(f32[16,16,64,2]{3,2,1,0:T(8,128)} %copy.66) | data formatting | bytes 262144
  85.3 0.1 rev.46
  85.4 1.3 %collective-permute-start.11 = (f32[8,8,4]{2,0,1:T(8,128)S(1)}, f32[8,8,4]{2,0,1:T(8,128)S(1)}, u32[]{:S(2)}, u32[]{:S(2)}) collective-permute-start(f32[8,8,4]{2,0,1:T(8,128)S(1)} %get-tuple-element.41), channel_id=1, source_target_pairs={{8,0},{16,8},{24,16},{32,24},{40,32},{48,40},{56,48},{9,1},{17,9},... | collective-permute-start | bytes 3080 | tf_op jit(solution)/shard_map/ppermute | solution.py:21
  86.7 0.1 rev.47
  86.8 6.0 %collective-permute-done.11 = f32[8,8,4]{2,0,1:T(8,128)S(1)} collective-permute-done((f32[8,8,4]{2,0,1:T(8,128)S(1)}, f32[8,8,4]{2,0,1:T(8,128)S(1)}, u32[]{:S(2)}, u32[]{:S(2)}) %collective-permute-start.11) | collective-permute-done | bytes 1056 | tf_op jit(solution)/shard_map/ppermute | solution.py:21
  92.8 0.1 pad_maximum_fusion.11
  92.9 0.2 copy.74
  93.3 1.6 %copy.77 = f32[8,8,32,2]{3,2,1,0:T(8,128)S(1)} copy(f32[8,8,32,2]{1,0,2,3:T(8,128)S(1)} %pad_maximum_fusion.2) | data formatting | bytes 32768 | tf_op jit(solution)/shard_map/stack | solution.py:51
  94.8 0.5 reshape.97
  95.3 15.6 %scatter_fusion = f32[32768]{0:T(1024)S(1)} fusion(f32[32768]{0:T(1024)S(1)} %reshape.73, s32[4096]{0:T(1024)S(1)} %reshape.95, f32[4096]{0:T(1024)S(1)} %reshape.97), kind=kCustom, calls=%fused_computation | custom fusion | bytes 65536
  110.9 0.0 copy-start
  110.9 0.6 copy-done
  (56 shorter events, 0.6 us)
Async XLA Ops:
  0.8 6.8 %collective-permute-start = (f32[4,16,128]{2,1,0:T(8,128)S(1)}, f32[4,16,128]{2,1,0:T(8,128)S(1)}, u32[]{:S(2)}, u32[]{:S(2)}) collective-permute-start(f32[4,16,128]{2,1,0:T(8,128)S(1)} %get-tuple-element.32), channel_id=1, source_target_pairs={{0,64},{64,128},{128,192},{192,256},{256,320},{320,384},{384,448},... | collective-permute-start | bytes 98312 | tf_op jit(solution)/shard_map/ppermute | solution.py:18
  5.7 6.4 %collective-permute-start.1 = (f32[4,16,128]{2,1,0:T(8,128)S(1)}, f32[4,16,128]{2,1,0:T(8,128)S(1)}, u32[]{:S(2)}, u32[]{:S(2)}) collective-permute-start(f32[4,16,128]{2,1,0:T(8,128)S(1)} %get-tuple-element.33), channel_id=1, source_target_pairs={{64,0},{128,64},{192,128},{256,192},{320,256},{384,320},{448,384},... | collective-permute-start | bytes 98312 | tf_op jit(solution)/shard_map/ppermute | solution.py:21
  14.0 5.3 %collective-permute-start.2 = (f32[16,4,128]{2,0,1:T(8,128)S(1)}, f32[16,4,128]{2,0,1:T(8,128)S(1)}, u32[]{:S(2)}, u32[]{:S(2)}) collective-permute-start(f32[16,4,128]{2,0,1:T(8,128)S(1)} %get-tuple-element.29), channel_id=1, source_target_pairs={{0,1},{1,2},{2,3},{3,4},{4,5},{5,6},{6,7},{8,9},{9,10},{10,11},{11... | collective-permute-start | bytes 98312 | tf_op jit(solution)/shard_map/ppermute | solution.py:18
  17.3 5.8 %collective-permute-start.3 = (f32[16,4,128]{2,0,1:T(8,128)S(1)}, f32[16,4,128]{2,0,1:T(8,128)S(1)}, u32[]{:S(2)}, u32[]{:S(2)}) collective-permute-start(f32[16,4,128]{2,0,1:T(8,128)S(1)} %get-tuple-element.27), channel_id=1, source_target_pairs={{1,0},{2,1},{3,2},{4,3},{5,4},{6,5},{7,6},{9,8},{10,9},{11,10},{12... | collective-permute-start | bytes 98312 | tf_op jit(solution)/shard_map/ppermute | solution.py:21
  23.5 6.8 %collective-permute-start.4 = (f32[16,16,4]{2,0,1:T(8,128)S(1)}, f32[16,16,4]{2,0,1:T(8,128)S(1)}, u32[]{:S(2)}, u32[]{:S(2)}) collective-permute-start(f32[16,16,4]{2,0,1:T(8,128)S(1)} %get-tuple-element.22), channel_id=1, source_target_pairs={{0,8},{8,16},{16,24},{24,32},{32,40},{40,48},{48,56},{1,9},{9,17},... | collective-permute-start | bytes 12296 | tf_op jit(solution)/shard_map/ppermute | solution.py:18
  28.5 7.3 %collective-permute-start.5 = (f32[16,16,4]{2,0,1:T(8,128)S(1)}, f32[16,16,4]{2,0,1:T(8,128)S(1)}, u32[]{:S(2)}, u32[]{:S(2)}) collective-permute-start(f32[16,16,4]{2,0,1:T(8,128)S(1)} %get-tuple-element.23), channel_id=1, source_target_pairs={{8,0},{16,8},{24,16},{32,24},{40,32},{48,40},{56,48},{9,1},{17,9},... | collective-permute-start | bytes 12296 | tf_op jit(solution)/shard_map/ppermute | solution.py:21
  37.3 9.8 %copy-start.2 = (s32[3]{0:T(128)S(1)}, s32[3]{0:T(128)}, u32[]{:S(2)}) copy-start(s32[3]{0:T(128)} %constant.28) | copy-start | bytes 40
  42.7 6.9 %collective-permute-start.6 = (f32[4,8,64]{1,0,2:T(4,128)S(1)}, f32[4,8,64]{1,0,2:T(4,128)S(1)}, u32[]{:S(2)}, u32[]{:S(2)}) collective-permute-start(f32[4,8,64]{1,0,2:T(4,128)S(1)} %get-tuple-element.11), channel_id=1, source_target_pairs={{0,64},{64,128},{128,192},{192,256},{256,320},{320,384},{384,448},... | collective-permute-start | bytes 24584 | tf_op jit(solution)/shard_map/ppermute | solution.py:18
  47.5 12.6 %copy-start.1 = (s32[3]{0:T(128)S(1)}, s32[3]{0:T(128)}, u32[]{:S(2)}) copy-start(s32[3]{0:T(128)} %constant.11) | copy-start | bytes 40
  47.5 7.5 %collective-permute-start.7 = (f32[4,8,64]{1,0,2:T(4,128)S(1)}, f32[4,8,64]{1,0,2:T(4,128)S(1)}, u32[]{:S(2)}, u32[]{:S(2)}) collective-permute-start(f32[4,8,64]{1,0,2:T(4,128)S(1)} %get-tuple-element.12), channel_id=1, source_target_pairs={{64,0},{128,64},{192,128},{256,192},{320,256},{384,320},{448,384},... | collective-permute-start | bytes 24584 | tf_op jit(solution)/shard_map/ppermute | solution.py:21
  55.2 6.9 %collective-permute-start.8 = (f32[8,4,64]{2,0,1:T(8,128)S(1)}, f32[8,4,64]{2,0,1:T(8,128)S(1)}, u32[]{:S(2)}, u32[]{:S(2)}) collective-permute-start(f32[8,4,64]{2,0,1:T(8,128)S(1)} %get-tuple-element.47), channel_id=1, source_target_pairs={{0,1},{1,2},{2,3},{3,4},{4,5},{5,6},{6,7},{8,9},{9,10},{10,11},{11... | collective-permute-start | bytes 24584 | tf_op jit(solution)/shard_map/ppermute | solution.py:18
  60.2 4.5 %collective-permute-start.9 = (f32[8,4,64]{2,0,1:T(8,128)S(1)}, f32[8,4,64]{2,0,1:T(8,128)S(1)}, u32[]{:S(2)}, u32[]{:S(2)}) collective-permute-start(f32[8,4,64]{2,0,1:T(8,128)S(1)} %get-tuple-element.45), channel_id=1, source_target_pairs={{1,0},{2,1},{3,2},{4,3},{5,4},{6,5},{7,6},{9,8},{10,9},{11,10},{12... | collective-permute-start | bytes 24584 | tf_op jit(solution)/shard_map/ppermute | solution.py:21
  64.9 21.8 %collective-permute-start.10 = (f32[8,8,4]{2,0,1:T(8,128)S(1)}, f32[8,8,4]{2,0,1:T(8,128)S(1)}, u32[]{:S(2)}, u32[]{:S(2)}) collective-permute-start(f32[8,8,4]{2,0,1:T(8,128)S(1)} %get-tuple-element.40), channel_id=1, source_target_pairs={{0,8},{8,16},{16,24},{24,32},{32,40},{40,48},{48,56},{1,9},{9,17},... | collective-permute-start | bytes 3080 | tf_op jit(solution)/shard_map/ppermute | solution.py:18
  85.4 7.4 %collective-permute-start.11 = (f32[8,8,4]{2,0,1:T(8,128)S(1)}, f32[8,8,4]{2,0,1:T(8,128)S(1)}, u32[]{:S(2)}, u32[]{:S(2)}) collective-permute-start(f32[8,8,4]{2,0,1:T(8,128)S(1)} %get-tuple-element.41), channel_id=1, source_target_pairs={{8,0},{16,8},{24,16},{32,24},{40,32},{48,40},{56,48},{9,1},{17,9},... | collective-permute-start | bytes 3080 | tf_op jit(solution)/shard_map/ppermute | solution.py:21
  110.9 0.7 copy-start
where the time goes:
time: 112 us
  local copies, waits for them, and re-layouts  42.5 us (38%)
  starting transfers between devices  37.4 us (33%)
  waiting for transfers between devices  28 us (25%)
  other arithmetic  2.96 us (3%)
    ppermute x6, waiting for transfers between devices, padded_2(): lax.ppermute(lax.slice_in_dim(block, 0, width, axis=dim), axis, backward)  27.6 us
    ppermute x6, starting transfers between devices, padded_2(): lax.ppermute(lax.slice_in_dim(block, block.shape[dim] - width, None, axis...  27.1 us
    unnamed x9, local copies, waits for them, and re-layouts  23.2 us
    ppermute x6, starting transfers between devices, padded_2(): lax.ppermute(lax.slice_in_dim(block, 0, width, axis=dim), axis, backward)  10.3 us
    another operation x6, local copies, waits for them, and re-layouts, lift_padded(): joined = jnp.stack([lowpass, highpass], axis=dim + 1)  10.3 us
    slice x2, local copies, waits for them, and re-layouts, on_device(): coarse = level_one[::2, ::2, ::2]  5.45 us
  transfers between devices with their start and end apart: 12, of which 7 were waited for; matrix products, arithmetic and copies ran while one was open for 15% of the time, Pallas kernels for 0%

commit v1 on v0

v1 whole, which is shorter than its diff:
```python
import jax
import jax.numpy as jnp
import numpy as np
from jax import lax
from jax.experimental import pallas as pl
from jax.experimental.pallas import tpu as pltpu
from jax.sharding import PartitionSpec as P

ALPHA = -1.586134342
BETA = -0.05298011854
GAMMA = 0.8829110762
DELTA = 0.4435068522
ZETA = 1.149604398

BLOCK = 16
LANES = 128
EDGE = 16


def lift_rows(rows, first, last):
    state = dict(rows)
    lo = first + (first & 1)
    hi = last - (last & 1)
    reach = 1
    for parity, weight in ((1, ALPHA), (0, BETA), (1, GAMMA), (0, DELTA)):
        for i in range(lo + reach, hi - reach + 1):
            if (i & 1) == parity:
                state[i] = state[i] + weight * (state[i - 1] + state[i + 1])
        reach += 1
    return state, lo + 4, hi - 4


def both_levels(rows, low, high, is_last):
    state, start, stop = lift_rows(rows, -low, BLOCK - 1 + high)
    coarse = {i // 2: state[i] * ZETA for i in range(start, stop + 1) if not i & 1}
    return coarse, second_level(coarse, is_last)


def second_level(coarse, is_last):
    half = BLOCK // 2
    coarse = dict(coarse)
    for j in range(3):
        coarse[half + j] = jnp.where(is_last, coarse[half - 2 - j], coarse[half + j])
    state, _, _ = lift_rows(coarse, -4, half + 2)
    return finish(state, half)


def finish(state, count):
    return [state[i] * (1.0 / ZETA) if i & 1 else state[i] * ZETA for i in range(count)]


def lift_matrix(padded):
    even, odd = padded[0::2], padded[1::2]
    odd = odd[:-1] + ALPHA * (even[:-1] + even[1:])
    even = even[1:-1] + BETA * (odd[:-1] + odd[1:])
    odd = odd[1:-1] + GAMMA * (even[:-1] + even[1:])
    even = even[1:-1] + DELTA * (odd[:-1] + odd[1:])
    out = np.zeros((2 * len(even), padded.shape[1]))
    out[0::2] = even * ZETA
    out[1::2] = odd[1:] / ZETA
    return out


def y_matrices():
    n, wide = LANES, 24
    size = n + 2 * wide
    eye = np.eye(size)
    own = eye[wide : wide + n]

    def levels(ext, last):
        one = lift_matrix(ext)
        low = one[0::2]
        if last:
            half = n // 2
            low = low.copy()
            for j in range(8):
                low[10 + half + j] = low[10 + half - 2 - j]
        two = lift_matrix(low[: len(low) - len(low) % 2])
        fine = np.zeros((n, size))
        fine[0::2] = two[6 : 6 + n // 2]
        return one[20 : 20 + n], fine

    inner = levels(eye, False)
    left = eye.copy()
    left[:wide] = own[1 : wide + 1][::-1]
    first = levels(left, False)
    right = eye.copy()
    right[wide + n :] = own[n - 1 - wide : n - 1][::-1]
    final = levels(right, True)
    mains, edges = [], []
    for a, b, c in zip(inner, first, final):
        a, b, c = a.T, b.T, c.T
        mid = a[wide : wide + n]
        edges.append(
            np.stack(
                [
                    a[wide - EDGE : wide],
                    (b - a)[wide : wide + EDGE],
                    a[wide + n : wide + n + EDGE],
                    (c - a)[wide + n - EDGE : wide + n],
                ]
            )
        )
        mains.append(mid)
    return np.stack(mains).astype(np.float32), np.stack(edges).astype(np.float32)


MAINS, EDGES = y_matrices()


def x_kernel(field, low, high, one, two, up, down):
    where = lax.axis_index("gx")
    is_first, is_last = where == 0, where == lax.axis_size("gx") - 1
    rows = {i: field[i] for i in range(BLOCK)}
    own = dict(rows)
    for k in range(1, 13):
        rows[-k] = jnp.where(is_first, own[k], low[12 - k])
    for k in range(1, 10):
        rows[BLOCK - 1 + k] = jnp.where(is_last, own[BLOCK - 1 - k], high[k - 1])
    state, _, _ = lift_rows(rows, -12, BLOCK + 8)
    coarse = {i // 2: state[i] * ZETA for i in range(-8, BLOCK + 5, 2)}
    for i, row in enumerate(finish(state, BLOCK)):
        one[i * BLOCK : (i + 1) * BLOCK, :] = row
    for i, row in enumerate(second_level(coarse, is_last)):
        two[i * BLOCK : (i + 1) * BLOCK, :] = row
    half = BLOCK // 2
    for j in range(4):
        up[j * BLOCK : (j + 1) * BLOCK, :] = one[pl.ds(BLOCK - 4 + j, BLOCK, stride=BLOCK), :]
    for j in range(12):
        up[4 * BLOCK + j * half : 4 * BLOCK + (j + 1) * half, :] = two[pl.ds(BLOCK - 12 + j, half, stride=BLOCK), :]
    for j in range(3):
        down[j * BLOCK : (j + 1) * BLOCK, :] = one[pl.ds(j, BLOCK, stride=BLOCK), :]
    for j in range(9):
        down[3 * BLOCK + j * half : 3 * BLOCK + (j + 1) * half, :] = two[pl.ds(j, half, stride=BLOCK), :]


def z_kernel(one, two, low, high, both, up, down):
    where = lax.axis_index("gz")
    is_first, is_last = where == 0, where == lax.axis_size("gz") - 1
    half = BLOCK // 2
    rows = {i: one[pl.ds(i, BLOCK, stride=BLOCK), :] for i in range(BLOCK)}
    own = dict(rows)
    for k in range(1, 5):
        rows[-k] = jnp.where(is_first, own[k], low[(4 - k) * BLOCK : (5 - k) * BLOCK, :])
    for k in range(1, 4):
        rows[BLOCK - 1 + k] = jnp.where(is_last, own[BLOCK - 1 - k], high[(k - 1) * BLOCK : k * BLOCK, :])
    state, _, _ = lift_rows(rows, -4, BLOCK + 2)
    parts = finish(state, BLOCK)
    rows = {i: two[pl.ds(i, half, stride=BLOCK), :] for i in range(BLOCK)}
    own = dict(rows)
    for k in range(1, 13):
        at = 4 * BLOCK + (12 - k) * half
        rows[-k] = jnp.where(is_first, own[k], low[at : at + half, :])
    for k in range(1, 10):
        at = 3 * BLOCK + (k - 1) * half
        rows[BLOCK - 1 + k] = jnp.where(is_last, own[BLOCK - 1 - k], high[at : at + half, :])
    state, _, _ = lift_rows(rows, -12, BLOCK + 8)
    coarse = {i // 2: state[i] * ZETA for i in range(-8, BLOCK + 5, 2)}
    parts += second_level(coarse, is_last)
    parts.append(jnp.zeros((64, LANES), jnp.float32))
    whole = jnp.concatenate(parts, axis=0)
    both[...] = whole
    turned = whole.T
    up[...] = turned[LANES - EDGE :, :]
    down[...] = turned[:EDGE, :]


def y_kernel(both, low, high, up, down, mains, edges, out):
    where = lax.axis_index("gy")
    is_first, is_last = where == 0, where == lax.axis_size("gy") - 1
    cells, half = BLOCK * BLOCK, BLOCK // 2
    ends = jnp.concatenate(
        [jnp.where(is_first, down[...], low[...]), jnp.where(is_last, up[...], high[...])], axis=0
    ).T

    def pass_y(k, start, stop):
        weights = jnp.concatenate(
            [jnp.where(is_first, edges[k, 1], edges[k, 0]), jnp.where(is_last, edges[k, 3], edges[k, 2])], axis=0
        )
        return jnp.dot(
            both[start:stop, :], mains[k], precision=lax.Precision.HIGHEST, preferred_element_type=jnp.float32
        ) + jnp.dot(
            ends[start:stop, :], weights, precision=lax.Precision.HIGHEST, preferred_element_type=jnp.float32
        )

    one = pass_y(0, 0, cells)
    two = pass_y(1, cells, cells + half * half)
    even = (lax.broadcasted_iota(jnp.int32, (half, LANES), 1) & 1) == 0
    for z in range(BLOCK):
        out[pl.ds(z, BLOCK, stride=BLOCK), :] = one[z * BLOCK : (z + 1) * BLOCK, :]
    for z in range(half):
        at = pl.ds(2 * z, half, stride=2 * BLOCK)
        out[at, :] = jnp.where(even, two[z * half : (z + 1) * half, :], out[at, :])


def call(kernel, shapes, *args):
    return pl.pallas_call(
        kernel,
        out_shape=[jax.ShapeDtypeStruct(s, jnp.float32) for s in shapes],
        name=kernel.__name__,
    )(*args)


def exchange(up, down, axis):
    count = lax.axis_size(axis)
    forward = [(i, i + 1) for i in range(count - 1)]
    backward = [(target, source) for source, target in forward]
    high = lax.ppermute(down, axis, backward)
    low = lax.ppermute(up, axis, forward)
    return low, high


def on_device(field):
    cells, half = BLOCK * BLOCK, BLOCK // 2
    low, high = exchange(field[BLOCK - 12 :], field[:9], "gx")
    one, two, up, down = call(
        x_kernel,
        [(cells, LANES), (half * BLOCK, LANES), (4 * BLOCK + 12 * half, LANES), (3 * BLOCK + 9 * half, LANES)],
        field,
        low,
        high,
    )
    low, high = exchange(up, down, "gz")
    wide = cells + 128
    both, up, down = call(z_kernel, [(wide, LANES), (EDGE, wide), (EDGE, wide)], one, two, low, high)
    low, high = exchange(up, down, "gy")
    (out,) = call(y_kernel, [(cells, LANES)], both, low, high, up, down, jnp.asarray(MAINS), jnp.asarray(EDGES))
    return out.reshape(BLOCK, BLOCK, LANES)


def solution(mesh):
    placed = (P("gx", "gz", "gy"),)
    return jax.shard_map(
        on_device, mesh=mesh, in_specs=placed, out_specs=P("gx", "gz", "gy"), check_vma=False
    )
```

time: 112 us -> 44.8 us (0.40)
  the two profiles are of different devices: /device:TPU:39 before, /device:TPU:311 now
where the time goes in v1:
time: 44.8 us; the launch traced here: 44.5 us
  starting transfers between devices  20.1 us (45%)
  waiting for transfers between devices  15 us (33%)
  Pallas kernels  5.88 us (13%)
  local copies, waits for them, and re-layouts  3.49 us (8%)
    ppermute x3, waiting for transfers between devices, exchange(): high = lax.ppermute(down, axis, backward)  15 us
    ppermute x3, starting transfers between devices, exchange(): low = lax.ppermute(up, axis, forward)  14.3 us
    pallas_call x3, Pallas kernels, call(): pl.pallas_call(kernel, out_shape=[jax.ShapeDtypeStruct(s, jnp.float32) fo...  5.88 us
    ppermute x3, starting transfers between devices, exchange(): high = lax.ppermute(down, axis, backward)  5.76 us
    unnamed x14, local copies, waits for them, and re-layouts  2.51 us
    slice x2, local copies, waits for them, and re-layouts, on_device(): low, high = exchange(field[BLOCK - 12:], field[:9], 'gx')  0.98 us
  transfers between devices with their start and end apart: 6, of which 3 were waited for; matrix products, arithmetic and copies ran while one was open for 0% of the time, Pallas kernels for 0%

profile of v1, /device:TPU:311, one launch (start us, length us, event | category | flops | bytes accessed | tf_op | source)
XLA Modules:
  0.0 44.5 jit_solution(11678329313621866837)
XLA Ops:
  0.0 0.0 copy-start
  0.0 1.0 %slice.6 = f32[12,16,128]{2,1,0:T(8,128)S(1)} slice(f32[16,16,128]{2,1,0:T(8,128)} %field.1), slice={[4:16], [0:16], [0:128]} | slice | bytes 196608 | tf_op jit(solution)/shard_map/slice | solution.py:215
  1.0 4.9 %collective-permute-start = (f32[12,16,128]{2,1,0:T(8,128)S(1)}, f32[12,16,128]{2,1,0:T(8,128)S(1)}, u32[]{:S(2)}, u32[]{:S(2)}) collective-permute-start(f32[12,16,128]{2,1,0:T(8,128)S(1)} %slice.6), channel_id=1, source_target_pairs={{0,64},{64,128},{128,192},{192,256},{256,320},{320,384},{384,448},... | collective-permute-start | bytes 294920 | tf_op jit(solution)/shard_map/ppermute | solution.py:209
  5.9 0.0 copy-done
  5.9 1.9 %collective-permute-start.1 = (f32[9,16,128]{2,1,0:T(8,128)S(1)}, f32[9,16,128]{2,1,0:T(8,128)S(1)}, u32[]{:S(2)}, u32[]{:S(2)}) collective-permute-start(f32[9,16,128]{2,1,0:T(8,128)S(1)} %slice.7), channel_id=1, source_target_pairs={{64,0},{128,64},{192,128},{256,192},{320,256},{384,320},{448,384},... | collective-permute-start | bytes 221192 | tf_op jit(solution)/shard_map/ppermute | solution.py:208
  7.8 5.0 %collective-permute-done.1.high = f32[9,16,128]{2,1,0:T(8,128)S(1)} collective-permute-done((f32[9,16,128]{2,1,0:T(8,128)S(1)}, f32[9,16,128]{2,1,0:T(8,128)S(1)}, u32[]{:S(2)}, u32[]{:S(2)}) %collective-permute-start.1) | collective-permute-done | bytes 73760 | tf_op jit(solution)/shard_map/ppermute | solution.py:208
  12.8 0.0 copy-start.3
  12.8 0.0 collective-permute-done.low
  12.8 0.6 %copy-done.3 = f32[9,16,128]{2,1,0:T(8,128)} copy-done((f32[9,16,128]{2,1,0:T(8,128)}, f32[9,16,128]{2,1,0:T(8,128)S(1)}, u32[]{:S(2)}) %copy-start.3) | copy-done | bytes 73752
  13.4 0.0 copy-start.1
  13.4 0.6 %copy-done.1 = f32[12,16,128]{2,1,0:T(8,128)} copy-done((f32[12,16,128]{2,1,0:T(8,128)}, f32[12,16,128]{2,1,0:T(8,128)S(1)}, u32[]{:S(2)}) %copy-start.1) | copy-done | bytes 98328
  14.0 1.8 %x_kernel.1 = (f32[256,128]{1,0:T(8,128)}, f32[128,128]{1,0:T(8,128)}, f32[160,128]{1,0:T(8,128)}, f32[120,128]{1,0:T(8,128)}) custom-call(f32[16,16,128]{2,1,0:T(8,128)} %field.1, f32[12,16,128]{2,1,0:T(8,128)} %copy-done.1, f32[9,16,128]{2,1,0:T(8,128)} %copy-done.3), custom_call_target="tpu_custom_call" | custom-call | tf_op jit(solution)/shard_map/x_kernel/pallas_call | solution.py:197
  15.8 4.5 %collective-permute-start.2 = (f32[160,128]{1,0:T(8,128)}, f32[160,128]{1,0:T(8,128)S(1)}, u32[]{:S(2)}, u32[]{:S(2)}) collective-permute-start(f32[160,128]{1,0:T(8,128)} %get-tuple-element.14), channel_id=1, source_target_pairs={{0,1},{1,2},{2,3},{3,4},{4,5},{5,6},{6,7},{8,9},{9,10},{10,11},{11... | collective-permute-start | bytes 245768 | tf_op jit(solution)/shard_map/ppermute | solution.py:209
  20.3 1.9 %collective-permute-start.3 = (f32[120,128]{1,0:T(8,128)}, f32[120,128]{1,0:T(8,128)S(1)}, u32[]{:S(2)}, u32[]{:S(2)}) collective-permute-start(f32[120,128]{1,0:T(8,128)} %get-tuple-element.15), channel_id=1, source_target_pairs={{1,0},{2,1},{3,2},{4,3},{5,4},{6,5},{7,6},{9,8},{10,9},{11,10},{12... | collective-permute-start | bytes 184328 | tf_op jit(solution)/shard_map/ppermute | solution.py:208
  22.3 4.5 %collective-permute-done.3.high = f32[120,128]{1,0:T(8,128)S(1)} collective-permute-done((f32[120,128]{1,0:T(8,128)}, f32[120,128]{1,0:T(8,128)S(1)}, u32[]{:S(2)}, u32[]{:S(2)}) %collective-permute-start.3) | collective-permute-done | bytes 61472 | tf_op jit(solution)/shard_map/ppermute | solution.py:208
  26.7 0.0 copy-start.4
  26.7 0.0 collective-permute-done.2.low
  26.7 0.0 copy-start.2
  26.7 0.6 %copy-done.4 = f32[120,128]{1,0:T(8,128)} copy-done((f32[120,128]{1,0:T(8,128)}, f32[120,128]{1,0:T(8,128)S(1)}, u32[]{:S(2)}) %copy-start.4) | copy-done | bytes 61464
  27.4 0.0 copy-done.2
  27.4 1.8 %z_kernel.1 = (f32[384,128]{1,0:T(8,128)}, f32[16,384]{1,0:T(8,128)}, f32[16,384]{1,0:T(8,128)}) custom-call(f32[256,128]{1,0:T(8,128)} %get-tuple-element.12.one, f32[128,128]{1,0:T(8,128)} %get-tuple-element.13.two, f32[160,128]{1,0:T(8,128)} %copy-done.2, f32[120,128]{1,0:T(8,128)} %copy-done.4), custom_call_target="tpu_custom_call" | custom-call | tf_op jit(solution)/shard_map/z_kernel/pallas_call | solution.py:197
  29.2 4.9 %collective-permute-start.4 = (f32[16,384]{1,0:T(8,128)}, f32[16,384]{1,0:T(8,128)S(1)}, u32[]{:S(2)}, u32[]{:S(2)}) collective-permute-start(f32[16,384]{1,0:T(8,128)} %get-tuple-element.17.up), channel_id=1, source_target_pairs={{0,8},{8,16},{16,24},{24,32},{32,40},{40,48},{48,56},{1,9},{9,17},... | collective-permute-start | bytes 73736 | tf_op jit(solution)/shard_map/ppermute | solution.py:209
  34.1 1.9 %collective-permute-start.5 = (f32[16,384]{1,0:T(8,128)}, f32[16,384]{1,0:T(8,128)S(1)}, u32[]{:S(2)}, u32[]{:S(2)}) collective-permute-start(f32[16,384]{1,0:T(8,128)} %get-tuple-element.18.down), channel_id=1, source_target_pairs={{8,0},{16,8},{24,16},{32,24},{40,32},{48,40},{56,48},{9,1},{17,9},... | collective-permute-start | bytes 73736 | tf_op jit(solution)/shard_map/ppermute | solution.py:208
  36.0 0.0 collective-permute-done.4.low
  36.1 0.0 copy-start.5
  36.1 5.6 %collective-permute-done.5.high = f32[16,384]{1,0:T(8,128)S(1)} collective-permute-done((f32[16,384]{1,0:T(8,128)}, f32[16,384]{1,0:T(8,128)S(1)}, u32[]{:S(2)}, u32[]{:S(2)}) %collective-permute-start.5) | collective-permute-done | bytes 24608 | tf_op jit(solution)/shard_map/ppermute | solution.py:208
  41.7 0.0 copy-start.6
  41.7 0.0 copy-done.5
  41.7 0.6 %copy-done.6 = f32[16,384]{1,0:T(8,128)} copy-done((f32[16,384]{1,0:T(8,128)}, f32[16,384]{1,0:T(8,128)S(1)}, u32[]{:S(2)}) %copy-start.6) | copy-done | bytes 24600
  42.3 2.3 %y_kernel.1 = f32[256,128]{1,0:T(8,128)} custom-call(f32[384,128]{1,0:T(8,128)} %get-tuple-element.16.both, f32[16,384]{1,0:T(8,128)} %copy-done.5, f32[16,384]{1,0:T(8,128)} %copy-done.6, f32[16,384]{1,0:T(8,128)} %get-tuple-element.17.up, f32[16,384]{1,0:T(8,128)} %get-tuple-element.18.down, f32[2,128,128]{2,1,0:T(8,128)} %constant.4.clone.mains, ...), custom_call_target="tpu_custom_call" | custom-call | tf_op jit(solution)/shard_map/y_kernel/pallas_call | solution.py:197
  (1 shorter events, 0.0 us)
Async XLA Ops:
  0.0 5.9 %copy-start = (f32[16,16,128]{2,1,0:T(8,128)S(1)}, f32[16,16,128]{2,1,0:T(8,128)}, u32[]{:S(2)}) copy-start(f32[16,16,128]{2,1,0:T(8,128)} %field.1) | copy-start | bytes 393220
  1.0 11.8 %collective-permute-start = (f32[12,16,128]{2,1,0:T(8,128)S(1)}, f32[12,16,128]{2,1,0:T(8,128)S(1)}, u32[]{:S(2)}, u32[]{:S(2)}) collective-permute-start(f32[12,16,128]{2,1,0:T(8,128)S(1)} %slice.6), channel_id=1, source_target_pairs={{0,64},{64,128},{128,192},{192,256},{256,320},{320,384},{384,448},... | collective-permute-start | bytes 294920 | tf_op jit(solution)/shard_map/ppermute | solution.py:209
  5.9 6.9 %collective-permute-start.1 = (f32[9,16,128]{2,1,0:T(8,128)S(1)}, f32[9,16,128]{2,1,0:T(8,128)S(1)}, u32[]{:S(2)}, u32[]{:S(2)}) collective-permute-start(f32[9,16,128]{2,1,0:T(8,128)S(1)} %slice.7), channel_id=1, source_target_pairs={{64,0},{128,64},{192,128},{256,192},{320,256},{384,320},{448,384},... | collective-permute-start | bytes 221192 | tf_op jit(solution)/shard_map/ppermute | solution.py:208
  12.8 0.6 %copy-start.3 = (f32[9,16,128]{2,1,0:T(8,128)}, f32[9,16,128]{2,1,0:T(8,128)S(1)}, u32[]{:S(2)}) copy-start(f32[9,16,128]{2,1,0:T(8,128)S(1)} %collective-permute-done.1.high) | copy-start | bytes 221188
  13.4 0.6 %copy-start.1 = (f32[12,16,128]{2,1,0:T(8,128)}, f32[12,16,128]{2,1,0:T(8,128)S(1)}, u32[]{:S(2)}) copy-start(f32[12,16,128]{2,1,0:T(8,128)S(1)} %collective-permute-done.low) | copy-start | bytes 294916
  15.8 10.9 %collective-permute-start.2 = (f32[160,128]{1,0:T(8,128)}, f32[160,128]{1,0:T(8,128)S(1)}, u32[]{:S(2)}, u32[]{:S(2)}) collective-permute-start(f32[160,128]{1,0:T(8,128)} %get-tuple-element.14), channel_id=1, source_target_pairs={{0,1},{1,2},{2,3},{3,4},{4,5},{5,6},{6,7},{8,9},{9,10},{10,11},{11... | collective-permute-start | bytes 245768 | tf_op jit(solution)/shard_map/ppermute | solution.py:209
  20.3 6.4 %collective-permute-start.3 = (f32[120,128]{1,0:T(8,128)}, f32[120,128]{1,0:T(8,128)S(1)}, u32[]{:S(2)}, u32[]{:S(2)}) collective-permute-start(f32[120,128]{1,0:T(8,128)} %get-tuple-element.15), channel_id=1, source_target_pairs={{1,0},{2,1},{3,2},{4,3},{5,4},{6,5},{7,6},{9,8},{10,9},{11,10},{12... | collective-permute-start | bytes 184328 | tf_op jit(solution)/shard_map/ppermute | solution.py:208
  26.7 0.6 %copy-start.4 = (f32[120,128]{1,0:T(8,128)}, f32[120,128]{1,0:T(8,128)S(1)}, u32[]{:S(2)}) copy-start(f32[120,128]{1,0:T(8,128)S(1)} %collective-permute-done.3.high) | copy-start | bytes 184324
  26.7 0.7 %copy-start.2 = (f32[160,128]{1,0:T(8,128)}, f32[160,128]{1,0:T(8,128)S(1)}, u32[]{:S(2)}) copy-start(f32[160,128]{1,0:T(8,128)S(1)} %collective-permute-done.2.low) | copy-start | bytes 245764
  29.2 6.8 %collective-permute-start.4 = (f32[16,384]{1,0:T(8,128)}, f32[16,384]{1,0:T(8,128)S(1)}, u32[]{:S(2)}, u32[]{:S(2)}) collective-permute-start(f32[16,384]{1,0:T(8,128)} %get-tuple-element.17.up), channel_id=1, source_target_pairs={{0,8},{8,16},{16,24},{24,32},{32,40},{40,48},{48,56},{1,9},{9,17},... | collective-permute-start | bytes 73736 | tf_op jit(solution)/shard_map/ppermute | solution.py:209
  34.1 7.5 %collective-permute-start.5 = (f32[16,384]{1,0:T(8,128)}, f32[16,384]{1,0:T(8,128)S(1)}, u32[]{:S(2)}, u32[]{:S(2)}) collective-permute-start(f32[16,384]{1,0:T(8,128)} %get-tuple-element.18.down), channel_id=1, source_target_pairs={{8,0},{16,8},{24,16},{32,24},{40,32},{48,40},{56,48},{9,1},{17,9},... | collective-permute-start | bytes 73736 | tf_op jit(solution)/shard_map/ppermute | solution.py:208
  36.1 5.6 %copy-start.5 = (f32[16,384]{1,0:T(8,128)}, f32[16,384]{1,0:T(8,128)S(1)}, u32[]{:S(2)}) copy-start(f32[16,384]{1,0:T(8,128)S(1)} %collective-permute-done.4.low) | copy-start | bytes 73732
  41.7 0.6 %copy-start.6 = (f32[16,384]{1,0:T(8,128)}, f32[16,384]{1,0:T(8,128)S(1)}, u32[]{:S(2)}) copy-start(f32[16,384]{1,0:T(8,128)S(1)} %collective-permute-done.5.high) | copy-start | bytes 73732

commit v2 on v1

--- a/solution.py
+++ b/solution.py
@@ -28,12 +28,6 @@
                 state[i] = state[i] + weight * (state[i - 1] + state[i + 1])
         reach += 1
     return state, lo + 4, hi - 4
-
-
-def both_levels(rows, low, high, is_last):
-    state, start, stop = lift_rows(rows, -low, BLOCK - 1 + high)
-    coarse = {i // 2: state[i] * ZETA for i in range(start, stop + 1) if not i & 1}
-    return coarse, second_level(coarse, is_last)
 
 
 def second_level(coarse, is_last):
@@ -193,12 +187,13 @@
         out[at, :] = jnp.where(even, two[z * half : (z + 1) * half, :], out[at, :])
 
 
+def near(shape):
+    return pltpu.VMEM(shape, jnp.float32)
+
+
 def call(kernel, shapes, *args):
-    return pl.pallas_call(
-        kernel,
-        out_shape=[jax.ShapeDtypeStruct(s, jnp.float32) for s in shapes],
-        name=kernel.__name__,
-    )(*args)
+    args = [pltpu.with_memory_space_constraint(a, pltpu.VMEM) for a in args]
+    return pl.pallas_call(kernel, out_shape=shapes)(*args)
 
 
 def exchange(up, down, axis):
@@ -215,16 +210,31 @@
     low, high = exchange(field[BLOCK - 12 :], field[:9], "gx")
     one, two, up, down = call(
         x_kernel,
-        [(cells, LANES), (half * BLOCK, LANES), (4 * BLOCK + 12 * half, LANES), (3 * BLOCK + 9 * half, LANES)],
+        [
+            near((cells, LANES)),
+            near((half * BLOCK, LANES)),
+            near((4 * BLOCK + 12 * half, LANES)),
+            near((3 * BLOCK + 9 * half, LANES)),
+        ],
         field,
         low,
         high,
     )
     low, high = exchange(up, down, "gz")
     wide = cells + 128
-    both, up, down = call(z_kernel, [(wide, LANES), (EDGE, wide), (EDGE, wide)], one, two, low, high)
+    both, up, down = call(z_kernel, [near((wide, LANES)), near((EDGE, wide)), near((EDGE, wide))], one, two, low, high)
     low, high = exchange(up, down, "gy")
-    (out,) = call(y_kernel, [(cells, LANES)], both, low, high, up, down, jnp.asarray(MAINS), jnp.asarray(EDGES))
+    (out,) = call(
+        y_kernel,
+        [jax.ShapeDtypeStruct((cells, LANES), jnp.float32)],
+        both,
+        low,
+        high,
+        up,
+        down,
+        jnp.asarray(MAINS),
+        jnp.asarray(EDGES),
+    )
     return out.reshape(BLOCK, BLOCK, LANES)
 
 

time: 44.8 us -> 37.6 us (0.84)
  Pallas kernels: 5.88 us -> 1.55 us
  local copies, waits for them, and re-layouts: 3.49 us -> 0.99 us
    pallas_call x3, Pallas kernels: 5.88 us -> 1.55 us  [call(): return pl.pallas_call(kernel, out_shape=shapes)(*args)]
    unnamed x14 -> x6, local copies, waits for them, and re-layouts: 2.51 us -> 0.01 us
where the time goes in v2:
time: 37.6 us; the launch traced here: 37.3 us
  starting transfers between devices  20.1 us (53%)
  waiting for transfers between devices  14.6 us (39%)
  Pallas kernels  1.55 us (4%)
  local copies, waits for them, and re-layouts  0.99 us (3%)
    ppermute x3, waiting for transfers between devices, exchange(): high = lax.ppermute(down, axis, backward)  14.6 us
    ppermute x3, starting transfers between devices, exchange(): low = lax.ppermute(up, axis, forward)  14.3 us
    ppermute x3, starting transfers between devices, exchange(): high = lax.ppermute(down, axis, backward)  5.76 us
    pallas_call x3, Pallas kernels, call(): return pl.pallas_call(kernel, out_shape=shapes)(*args)  1.55 us
    slice x2, local copies, waits for them, and re-layouts, on_device(): low, high = exchange(field[BLOCK - 12:], field[:9], 'gx')  0.98 us
  transfers between devices with their start and end apart: 6, of which 3 were waited for; matrix products, arithmetic and copies ran while one was open for 0% of the time, Pallas kernels for 0%

profile of v2, /device:TPU:311, one launch (start us, length us, event | category | flops | bytes accessed | tf_op | source)
XLA Modules:
  0.0 37.3 jit_solution(8098352761335919121)
XLA Ops:
  0.0 0.0 copy-start
  0.0 1.0 %slice.6 = f32[12,16,128]{2,1,0:T(8,128)S(1)} slice(f32[16,16,128]{2,1,0:T(8,128)} %field.1), slice={[4:16], [0:16], [0:128]} | slice | bytes 196608 | tf_op jit(solution)/shard_map/slice | solution.py:210
  1.0 4.9 %collective-permute-start = (f32[12,16,128]{2,1,0:T(8,128)S(1)}, f32[12,16,128]{2,1,0:T(8,128)S(1)}, u32[]{:S(2)}, u32[]{:S(2)}) collective-permute-start(f32[12,16,128]{2,1,0:T(8,128)S(1)} %slice.6), channel_id=1, source_target_pairs={{0,64},{64,128},{128,192},{192,256},{256,320},{320,384},{384,448},... | collective-permute-start | bytes 294920 | tf_op jit(solution)/shard_map/ppermute | solution.py:204
  5.9 0.0 copy-done
  5.9 1.9 %collective-permute-start.1 = (f32[9,16,128]{2,1,0:T(8,128)S(1)}, f32[9,16,128]{2,1,0:T(8,128)S(1)}, u32[]{:S(2)}, u32[]{:S(2)}) collective-permute-start(f32[9,16,128]{2,1,0:T(8,128)S(1)} %slice.7), channel_id=1, source_target_pairs={{64,0},{128,64},{192,128},{256,192},{320,256},{384,320},{448,384},... | collective-permute-start | bytes 221192 | tf_op jit(solution)/shard_map/ppermute | solution.py:203
  7.8 5.0 %collective-permute-done.1.high = f32[9,16,128]{2,1,0:T(8,128)S(1)} collective-permute-done((f32[9,16,128]{2,1,0:T(8,128)S(1)}, f32[9,16,128]{2,1,0:T(8,128)S(1)}, u32[]{:S(2)}, u32[]{:S(2)}) %collective-permute-start.1) | collective-permute-done | bytes 73760 | tf_op jit(solution)/shard_map/ppermute | solution.py:203
  12.8 0.0 collective-permute-done.low
  12.8 0.1 shard_map.37
  12.9 4.5 %collective-permute-start.2 = (f32[160,128]{1,0:T(8,128)S(1)}, f32[160,128]{1,0:T(8,128)S(1)}, u32[]{:S(2)}, u32[]{:S(2)}) collective-permute-start(f32[160,128]{1,0:T(8,128)S(1)} %get-tuple-element.14), channel_id=1, source_target_pairs={{0,1},{1,2},{2,3},{3,4},{4,5},{5,6},{6,7},{8,9},{9,10},{10,11},{11... | collective-permute-start | bytes 245768 | tf_op jit(solution)/shard_map/ppermute | solution.py:204
  17.4 1.9 %collective-permute-start.3 = (f32[120,128]{1,0:T(8,128)S(1)}, f32[120,128]{1,0:T(8,128)S(1)}, u32[]{:S(2)}, u32[]{:S(2)}) collective-permute-start(f32[120,128]{1,0:T(8,128)S(1)} %get-tuple-element.15), channel_id=1, source_target_pairs={{1,0},{2,1},{3,2},{4,3},{5,4},{6,5},{7,6},{9,8},{10,9},{11,10},{12... | collective-permute-start | bytes 184328 | tf_op jit(solution)/shard_map/ppermute | solution.py:203
  19.4 4.2 %collective-permute-done.3.high = f32[120,128]{1,0:T(8,128)S(1)} collective-permute-done((f32[120,128]{1,0:T(8,128)S(1)}, f32[120,128]{1,0:T(8,128)S(1)}, u32[]{:S(2)}, u32[]{:S(2)}) %collective-permute-start.3) | collective-permute-done | bytes 61472 | tf_op jit(solution)/shard_map/ppermute | solution.py:203
  23.6 0.0 collective-permute-done.2.low
  23.6 0.0 copy-start.1
  23.6 0.0 copy-start.2
  23.6 0.2 shard_map.38
  23.8 4.9 %collective-permute-start.4 = (f32[16,384]{1,0:T(8,128)S(1)}, f32[16,384]{1,0:T(8,128)S(1)}, u32[]{:S(2)}, u32[]{:S(2)}) collective-permute-start(f32[16,384]{1,0:T(8,128)S(1)} %get-tuple-element.17.up), channel_id=1, source_target_pairs={{0,8},{8,16},{16,24},{24,32},{32,40},{40,48},{48,56},{1,9},{9,17},... | collective-permute-start | bytes 73736 | tf_op jit(solution)/shard_map/ppermute | solution.py:204
  28.8 1.9 %collective-permute-start.5 = (f32[16,384]{1,0:T(8,128)S(1)}, f32[16,384]{1,0:T(8,128)S(1)}, u32[]{:S(2)}, u32[]{:S(2)}) collective-permute-start(f32[16,384]{1,0:T(8,128)S(1)} %get-tuple-element.18.down), channel_id=1, source_target_pairs={{8,0},{16,8},{24,16},{32,24},{40,32},{48,40},{56,48},{9,1},{17,9},... | collective-permute-start | bytes 73736 | tf_op jit(solution)/shard_map/ppermute | solution.py:203
  30.7 0.0 collective-permute-done.4.low
  30.7 5.4 %collective-permute-done.5.high = f32[16,384]{1,0:T(8,128)S(1)} collective-permute-done((f32[16,384]{1,0:T(8,128)S(1)}, f32[16,384]{1,0:T(8,128)S(1)}, u32[]{:S(2)}, u32[]{:S(2)}) %collective-permute-start.5) | collective-permute-done | bytes 24608 | tf_op jit(solution)/shard_map/ppermute | solution.py:203
  36.1 0.0 copy-done.1
  36.1 0.0 copy-done.2
  36.1 1.2 %shard_map.39 = f32[256,128]{1,0:T(8,128)} custom-call(f32[384,128]{1,0:T(8,128)S(1)} %get-tuple-element.16.both, f32[16,384]{1,0:T(8,128)S(1)} %collective-permute-done.4.low, f32[16,384]{1,0:T(8,128)S(1)} %collective-permute-done.5.high, f32[16,384]{1,0:T(8,128)S(1)} %get-tuple-element.17.up, f32[16,384]{1,0:T(8,128)S(1)} %get-tuple-element.18.down, ...), custom_call_target="tpu_custom_call" | custom-call | tf_op jit(solution)/shard_map/pallas_call | solution.py:196
  (1 shorter events, 0.0 us)
Async XLA Ops:
  0.0 5.9 %copy-start = (f32[16,16,128]{2,1,0:T(8,128)S(1)}, f32[16,16,128]{2,1,0:T(8,128)}, u32[]{:S(2)}) copy-start(f32[16,16,128]{2,1,0:T(8,128)} %field.1) | copy-start | bytes 393220
  1.0 11.8 %collective-permute-start = (f32[12,16,128]{2,1,0:T(8,128)S(1)}, f32[12,16,128]{2,1,0:T(8,128)S(1)}, u32[]{:S(2)}, u32[]{:S(2)}) collective-permute-start(f32[12,16,128]{2,1,0:T(8,128)S(1)} %slice.6), channel_id=1, source_target_pairs={{0,64},{64,128},{128,192},{192,256},{256,320},{320,384},{384,448},... | collective-permute-start | bytes 294920 | tf_op jit(solution)/shard_map/ppermute | solution.py:204
  5.9 6.9 %collective-permute-start.1 = (f32[9,16,128]{2,1,0:T(8,128)S(1)}, f32[9,16,128]{2,1,0:T(8,128)S(1)}, u32[]{:S(2)}, u32[]{:S(2)}) collective-permute-start(f32[9,16,128]{2,1,0:T(8,128)S(1)} %slice.7), channel_id=1, source_target_pairs={{64,0},{128,64},{192,128},{256,192},{320,256},{384,320},{448,384},... | collective-permute-start | bytes 221192 | tf_op jit(solution)/shard_map/ppermute | solution.py:203
  12.9 10.7 %collective-permute-start.2 = (f32[160,128]{1,0:T(8,128)S(1)}, f32[160,128]{1,0:T(8,128)S(1)}, u32[]{:S(2)}, u32[]{:S(2)}) collective-permute-start(f32[160,128]{1,0:T(8,128)S(1)} %get-tuple-element.14), channel_id=1, source_target_pairs={{0,1},{1,2},{2,3},{3,4},{4,5},{5,6},{6,7},{8,9},{9,10},{10,11},{11... | collective-permute-start | bytes 245768 | tf_op jit(solution)/shard_map/ppermute | solution.py:204
  17.4 6.2 %collective-permute-start.3 = (f32[120,128]{1,0:T(8,128)S(1)}, f32[120,128]{1,0:T(8,128)S(1)}, u32[]{:S(2)}, u32[]{:S(2)}) collective-permute-start(f32[120,128]{1,0:T(8,128)S(1)} %get-tuple-element.15), channel_id=1, source_target_pairs={{1,0},{2,1},{3,2},{4,3},{5,4},{6,5},{7,6},{9,8},{10,9},{11,10},{12... | collective-permute-start | bytes 184328 | tf_op jit(solution)/shard_map/ppermute | solution.py:203
  23.6 12.5 %copy-start.1 = (f32[2,128,128]{2,1,0:T(8,128)S(1)}, f32[2,128,128]{2,1,0:T(8,128)}, u32[]{:S(2)}) copy-start(f32[2,128,128]{2,1,0:T(8,128)} %constant.4.clone.mains) | copy-start | bytes 393220
  23.6 12.5 %copy-start.2 = (f32[2,4,16,128]{3,2,1,0:T(8,128)S(1)}, f32[2,4,16,128]{3,2,1,0:T(8,128)}, u32[]{:S(2)}) copy-start(f32[2,4,16,128]{3,2,1,0:T(8,128)} %constant.5.clone.edges) | copy-start | bytes 196612
  23.8 6.8 %collective-permute-start.4 = (f32[16,384]{1,0:T(8,128)S(1)}, f32[16,384]{1,0:T(8,128)S(1)}, u32[]{:S(2)}, u32[]{:S(2)}) collective-permute-start(f32[16,384]{1,0:T(8,128)S(1)} %get-tuple-element.17.up), channel_id=1, source_target_pairs={{0,8},{8,16},{16,24},{24,32},{32,40},{40,48},{48,56},{1,9},{9,17},... | collective-permute-start | bytes 73736 | tf_op jit(solution)/shard_map/ppermute | solution.py:204
  28.8 7.3 %collective-permute-start.5 = (f32[16,384]{1,0:T(8,128)S(1)}, f32[16,384]{1,0:T(8,128)S(1)}, u32[]{:S(2)}, u32[]{:S(2)}) collective-permute-start(f32[16,384]{1,0:T(8,128)S(1)} %get-tuple-element.18.down), channel_id=1, source_target_pairs={{8,0},{16,8},{24,16},{32,24},{40,32},{48,40},{56,48},{9,1},{17,9},... | collective-permute-start | bytes 73736 | tf_op jit(solution)/shard_map/ppermute | solution.py:203

commit v3 on v2

--- a/solution.py
+++ b/solution.py
@@ -17,30 +17,59 @@
 EDGE = 16
 
 
-def lift_rows(rows, first, last):
-    state = dict(rows)
-    lo = first + (first & 1)
-    hi = last - (last & 1)
-    reach = 1
-    for parity, weight in ((1, ALPHA), (0, BETA), (1, GAMMA), (0, DELTA)):
-        for i in range(lo + reach, hi - reach + 1):
-            if (i & 1) == parity:
-                state[i] = state[i] + weight * (state[i - 1] + state[i + 1])
-        reach += 1
-    return state, lo + 4, hi - 4
-
-
-def second_level(coarse, is_last):
+STEPS = (ALPHA, BETA, GAMMA, DELTA)
+
+
+def advance(state, step, index):
+    before = max(step - 2, -1) if step > 1 else -1
+    side = step - 1
+    state[step, index] = state[before, index] + STEPS[step] * (state[side, index - 1] + state[side, index + 1])
+
+
+def lift(state, spans):
+    for step, (first, last) in enumerate(spans):
+        for index in range(first, last + 1, 2):
+            if (step, index) not in state:
+                advance(state, step, index)
+
+
+UP = ((-1, 15), (-1, 14), (0, 13), (1, 12), (2, 11), (3, 10), (3, 8))
+DOWN = ((-1, 0), (0, 1), (1, 2), (2, 3), (3, 4))
+MIRROR_LOW = ((-1, 1), (-1, 2), (0, 3), (1, 4), (2, 5), (3, 6), (3, 8))
+MIRROR_HIGH = ((-1, 14), (0, 13), (1, 12), (2, 11), (3, 10))
+INNER = ((1, 13), (2, 12), (3, 11), (4, 10))
+BOTH = ((-1, 15), (-2, 16), (-3, 17), (-4, 18))
+ONE = ((-1, 15), (-2, 16), (-1, 15), (0, 14))
+
+
+def started(rows):
+    state = {(-1, i): rows[i] for i in range(BLOCK)}
+    lift(state, INNER)
+    return state
+
+
+def joined(state, low, high, is_first, is_last, spans):
+    for k, value in enumerate(low):
+        step, index = UP[k]
+        state[step, index - BLOCK] = jnp.where(is_first, state[MIRROR_LOW[k]], value)
+    for k, value in enumerate(high):
+        step, index = DOWN[k]
+        state[step, index + BLOCK] = jnp.where(is_last, state[MIRROR_HIGH[k]], value)
+    lift(state, spans)
+    return state
+
+
+def level_one(state):
+    return [state[2, i] * (1.0 / ZETA) if i & 1 else state[3, i] * ZETA for i in range(BLOCK)]
+
+
+def level_two(state, is_last):
     half = BLOCK // 2
-    coarse = dict(coarse)
+    coarse = {(-1, i): state[3, 2 * i] * ZETA for i in range(-4, half + 3)}
     for j in range(3):
-        coarse[half + j] = jnp.where(is_last, coarse[half - 2 - j], coarse[half + j])
-    state, _, _ = lift_rows(coarse, -4, half + 2)
-    return finish(state, half)
-
-
-def finish(state, count):
-    return [state[i] * (1.0 / ZETA) if i & 1 else state[i] * ZETA for i in range(count)]
+        coarse[-1, half + j] = jnp.where(is_last, coarse[-1, half - 2 - j], coarse[-1, half + j])
+    lift(coarse, ((-3, half + 1), (-2, half), (-1, half - 1), (0, half - 2)))
+    return [coarse[2, i] * (1.0 / ZETA) if i & 1 else coarse[3, i] * ZETA for i in range(half)]
 
 
 def lift_matrix(padded):
@@ -102,56 +131,51 @@
 MAINS, EDGES = y_matrices()
 
 
+def blank_kernel(blank):
+    blank[...] = jnp.zeros(blank.shape, jnp.float32)
+
+
+def x_start_kernel(field, blank, down):
+    state = started({i: field[i] for i in range(BLOCK)})
+    for k, key in enumerate(DOWN):
+        down[k] = state[key]
+
+
 def x_kernel(field, low, high, one, two, up, down):
     where = lax.axis_index("gx")
     is_first, is_last = where == 0, where == lax.axis_size("gx") - 1
-    rows = {i: field[i] for i in range(BLOCK)}
-    own = dict(rows)
-    for k in range(1, 13):
-        rows[-k] = jnp.where(is_first, own[k], low[12 - k])
-    for k in range(1, 10):
-        rows[BLOCK - 1 + k] = jnp.where(is_last, own[BLOCK - 1 - k], high[k - 1])
-    state, _, _ = lift_rows(rows, -12, BLOCK + 8)
-    coarse = {i // 2: state[i] * ZETA for i in range(-8, BLOCK + 5, 2)}
-    for i, row in enumerate(finish(state, BLOCK)):
+    half = BLOCK // 2
+    before = started({i: low[i] for i in range(BLOCK)})
+    state = started({i: field[i] for i in range(BLOCK)})
+    joined(state, [before[key] for key in UP], [high[k] for k in range(len(DOWN))], is_first, is_last, BOTH)
+    for i, row in enumerate(level_one(state)):
         one[i * BLOCK : (i + 1) * BLOCK, :] = row
-    for i, row in enumerate(second_level(coarse, is_last)):
+    for i, row in enumerate(level_two(state, is_last)):
         two[i * BLOCK : (i + 1) * BLOCK, :] = row
-    half = BLOCK // 2
-    for j in range(4):
-        up[j * BLOCK : (j + 1) * BLOCK, :] = one[pl.ds(BLOCK - 4 + j, BLOCK, stride=BLOCK), :]
-    for j in range(12):
-        up[4 * BLOCK + j * half : 4 * BLOCK + (j + 1) * half, :] = two[pl.ds(BLOCK - 12 + j, half, stride=BLOCK), :]
-    for j in range(3):
-        down[j * BLOCK : (j + 1) * BLOCK, :] = one[pl.ds(j, BLOCK, stride=BLOCK), :]
-    for j in range(9):
-        down[3 * BLOCK + j * half : 3 * BLOCK + (j + 1) * half, :] = two[pl.ds(j, half, stride=BLOCK), :]
-
-
-def z_kernel(one, two, low, high, both, up, down):
+    for source, count, ups, downs in ((one, BLOCK, 3, 2), (two, half, 7, 5)):
+        state = started({i: source[pl.ds(i, count, stride=BLOCK), :] for i in range(BLOCK)})
+        base = 0 if count == BLOCK else 3 * BLOCK
+        for k in range(ups):
+            up[base + k * count : base + (k + 1) * count, :] = state[UP[k]]
+        base = 0 if count == BLOCK else 2 * BLOCK
+        for k in range(downs):
+            down[base + k * count : base + (k + 1) * count, :] = state[DOWN[k]]
+
+
+def z_kernel(one, two, low, high, blank, both, up, down):
     where = lax.axis_index("gz")
     is_first, is_last = where == 0, where == lax.axis_size("gz") - 1
     half = BLOCK // 2
-    rows = {i: one[pl.ds(i, BLOCK, stride=BLOCK), :] for i in range(BLOCK)}
-    own = dict(rows)
-    for k in range(1, 5):
-        rows[-k] = jnp.where(is_first, own[k], low[(4 - k) * BLOCK : (5 - k) * BLOCK, :])
-    for k in range(1, 4):
-        rows[BLOCK - 1 + k] = jnp.where(is_last, own[BLOCK - 1 - k], high[(k - 1) * BLOCK : k * BLOCK, :])
-    state, _, _ = lift_rows(rows, -4, BLOCK + 2)
-    parts = finish(state, BLOCK)
-    rows = {i: two[pl.ds(i, half, stride=BLOCK), :] for i in range(BLOCK)}
-    own = dict(rows)
-    for k in range(1, 13):
-        at = 4 * BLOCK + (12 - k) * half
-        rows[-k] = jnp.where(is_first, own[k], low[at : at + half, :])
-    for k in range(1, 10):
-        at = 3 * BLOCK + (k - 1) * half
-        rows[BLOCK - 1 + k] = jnp.where(is_last, own[BLOCK - 1 - k], high[at : at + half, :])
-    state, _, _ = lift_rows(rows, -12, BLOCK + 8)
-    coarse = {i // 2: state[i] * ZETA for i in range(-8, BLOCK + 5, 2)}
-    parts += second_level(coarse, is_last)
-    parts.append(jnp.zeros((64, LANES), jnp.float32))
+    parts = []
+    for source, count, ups, downs, spans in ((one, BLOCK, 3, 2, ONE), (two, half, 7, 5, BOTH)):
+        state = started({i: source[pl.ds(i, count, stride=BLOCK), :] for i in range(BLOCK)})
+        base = 0 if count == BLOCK else 3 * BLOCK
+        lows = [low[base + k * count : base + (k + 1) * count, :] for k in range(ups)]
+        base = 0 if count == BLOCK else 2 * BLOCK
+        highs = [high[base + k * count : base + (k + 1) * count, :] for k in range(downs)]
+        joined(state, lows, highs, is_first, is_last, spans)
+        parts += level_one(state) if count == BLOCK else level_two(state, is_last)
+    parts.append(blank[...])
     whole = jnp.concatenate(parts, axis=0)
     both[...] = whole
     turned = whole.T
@@ -191,9 +215,10 @@
     return pltpu.VMEM(shape, jnp.float32)
 
 
-def call(kernel, shapes, *args):
+def call(kernel, shapes, *args, flops=None):
     args = [pltpu.with_memory_space_constraint(a, pltpu.VMEM) for a in args]
-    return pl.pallas_call(kernel, out_shape=shapes)(*args)
+    cost = None if flops is None else pl.CostEstimate(flops=flops, bytes_accessed=4096, transcendentals=0)
+    return pl.pallas_call(kernel, out_shape=shapes, cost_estimate=cost)(*args)
 
 
 def exchange(up, down, axis):
@@ -207,14 +232,16 @@
 
 def on_device(field):
     cells, half = BLOCK * BLOCK, BLOCK // 2
-    low, high = exchange(field[BLOCK - 12 :], field[:9], "gx")
+    (blank,) = call(blank_kernel, [near((64, LANES))], flops=10**8)
+    (down,) = call(x_start_kernel, [near((len(DOWN), BLOCK, LANES))], field, blank)
+    low, high = exchange(field, down, "gx")
     one, two, up, down = call(
         x_kernel,
         [
             near((cells, LANES)),
             near((half * BLOCK, LANES)),
-            near((4 * BLOCK + 12 * half, LANES)),
-            near((3 * BLOCK + 9 * half, LANES)),
+            near((3 * BLOCK + 7 * half, LANES)),
+            near((2 * BLOCK + 5 * half, LANES)),
         ],
         field,
         low,
@@ -222,7 +249,9 @@
     )
     low, high = exchange(up, down, "gz")
     wide = cells + 128
-    both, up, down = call(z_kernel, [near((wide, LANES)), near((EDGE, wide)), near((EDGE, wide))], one, two, low, high)
+    both, up, down = call(
+        z_kernel, [near((wide, LANES)), near((EDGE, wide)), near((EDGE, wide))], one, two, low, high, blank
+    )
     low, high = exchange(up, down, "gy")
     (out,) = call(
         y_kernel,

time: 37.6 us -> 36.1 us (0.960)
  local copies, waits for them, and re-layouts: 0.99 us -> 0.01 us
  waiting for transfers between devices: 14.6 us -> 14 us
    slice x2 -> x0, local copies, waits for them, and re-layouts: 0.98 us -> none  [on_device(): low, high = exchange(field[BLOCK - 12:], field[:9], 'gx')]
    ppermute x3, waiting for transfers between devices: 14.6 us -> 14 us  [exchange(): high = lax.ppermute(down, axis, backward)]
    pallas_call x3 -> x5, Pallas kernels: 1.55 us -> 1.54 us  [call(): return pl.pallas_call(kernel, out_shape=shapes, cost_estimate=cost)(*args)]
where the time goes in v3:
time: 36.1 us; the launch traced here: 35.9 us
  starting transfers between devices  20.2 us (56%)
  waiting for transfers between devices  14 us (39%)
  Pallas kernels  1.54 us (4%)
    ppermute x3, starting transfers between devices, exchange(): low = lax.ppermute(up, axis, forward)  14.5 us
    ppermute x3, waiting for transfers between devices, exchange(): high = lax.ppermute(down, axis, backward)  14 us
    ppermute x3, starting transfers between devices, exchange(): high = lax.ppermute(down, axis, backward)  5.76 us
    pallas_call x5, Pallas kernels, call(): return pl.pallas_call(kernel, out_shape=shapes, cost_estimate=cost)(*args)  1.54 us
  transfers between devices with their start and end apart: 6, of which 3 were waited for; matrix products, arithmetic and copies ran while one was open for 0% of the time, Pallas kernels for 0%

profile of v3, /device:TPU:311, one launch (start us, length us, event | category | flops | bytes accessed | tf_op | source)
XLA Modules:
  0.0 35.9 jit_solution(7938254987502404064)
XLA Ops:
  0.0 0.0 copy-start
  0.0 5.0 %collective-permute-start = (f32[16,16,128]{2,1,0:T(8,128)}, f32[16,16,128]{2,1,0:T(8,128)S(1)}, u32[]{:S(2)}, u32[]{:S(2)}) collective-permute-start(f32[16,16,128]{2,1,0:T(8,128)} %field.3), channel_id=1, source_target_pairs={{0,64},{64,128},{128,192},{192,256},{256,320},{320,384},{384,448},... | collective-permute-start | bytes 393224 | tf_op jit(solution)/shard_map/ppermute | solution.py:229
  5.0 0.0 copy-done
  5.1 1.9 %collective-permute-start.1 = (f32[5,16,128]{2,1,0:T(8,128)S(1)}, f32[5,16,128]{2,1,0:T(8,128)S(1)}, u32[]{:S(2)}, u32[]{:S(2)}) collective-permute-start(f32[5,16,128]{2,1,0:T(8,128)S(1)} %shard_map.38), channel_id=1, source_target_pairs={{64,0},{128,64},{192,128},{256,192},{320,256},{384,320},{448,384},... | collective-permute-start | bytes 122888 | tf_op jit(solution)/shard_map/ppermute | solution.py:228
  7.0 4.6 %collective-permute-done.1.high = f32[5,16,128]{2,1,0:T(8,128)S(1)} collective-permute-done((f32[5,16,128]{2,1,0:T(8,128)S(1)}, f32[5,16,128]{2,1,0:T(8,128)S(1)}, u32[]{:S(2)}, u32[]{:S(2)}) %collective-permute-start.1) | collective-permute-done | bytes 40992 | tf_op jit(solution)/shard_map/ppermute | solution.py:228
  11.6 0.0 collective-permute-done.low
  11.6 0.1 shard_map.39
  11.7 4.5 %collective-permute-start.2 = (f32[104,128]{1,0:T(8,128)S(1)}, f32[104,128]{1,0:T(8,128)S(1)}, u32[]{:S(2)}, u32[]{:S(2)}) collective-permute-start(f32[104,128]{1,0:T(8,128)S(1)} %get-tuple-element.14), channel_id=1, source_target_pairs={{0,1},{1,2},{2,3},{3,4},{4,5},{5,6},{6,7},{8,9},{9,10},{10,11},{11... | collective-permute-start | bytes 159752 | tf_op jit(solution)/shard_map/ppermute | solution.py:229
  16.3 1.9 %collective-permute-start.3 = (f32[72,128]{1,0:T(8,128)S(1)}, f32[72,128]{1,0:T(8,128)S(1)}, u32[]{:S(2)}, u32[]{:S(2)}) collective-permute-start(f32[72,128]{1,0:T(8,128)S(1)} %get-tuple-element.15), channel_id=1, source_target_pairs={{1,0},{2,1},{3,2},{4,3},{5,4},{6,5},{7,6},{9,8},{10,9},{11,10},{12... | collective-permute-start | bytes 110600 | tf_op jit(solution)/shard_map/ppermute | solution.py:228
  18.2 4.0 %collective-permute-done.3.high = f32[72,128]{1,0:T(8,128)S(1)} collective-permute-done((f32[72,128]{1,0:T(8,128)S(1)}, f32[72,128]{1,0:T(8,128)S(1)}, u32[]{:S(2)}, u32[]{:S(2)}) %collective-permute-start.3) | collective-permute-done | bytes 36896 | tf_op jit(solution)/shard_map/ppermute | solution.py:228
  22.2 0.0 collective-permute-done.2.low
  22.2 0.0 copy-start.1
  22.2 0.0 copy-start.2
  22.2 0.2 shard_map.40
  22.4 4.9 %collective-permute-start.4 = (f32[16,384]{1,0:T(8,128)S(1)}, f32[16,384]{1,0:T(8,128)S(1)}, u32[]{:S(2)}, u32[]{:S(2)}) collective-permute-start(f32[16,384]{1,0:T(8,128)S(1)} %get-tuple-element.17.up), channel_id=1, source_target_pairs={{0,8},{8,16},{16,24},{24,32},{32,40},{40,48},{48,56},{1,9},{9,17},... | collective-permute-start | bytes 73736 | tf_op jit(solution)/shard_map/ppermute | solution.py:229
  27.3 1.9 %collective-permute-start.5 = (f32[16,384]{1,0:T(8,128)S(1)}, f32[16,384]{1,0:T(8,128)S(1)}, u32[]{:S(2)}, u32[]{:S(2)}) collective-permute-start(f32[16,384]{1,0:T(8,128)S(1)} %get-tuple-element.18.down), channel_id=1, source_target_pairs={{8,0},{16,8},{24,16},{32,24},{40,32},{48,40},{56,48},{9,1},{17,9},... | collective-permute-start | bytes 73736 | tf_op jit(solution)/shard_map/ppermute | solution.py:228
  29.2 0.0 collective-permute-done.4.low
  29.3 5.4 %collective-permute-done.5.high = f32[16,384]{1,0:T(8,128)S(1)} collective-permute-done((f32[16,384]{1,0:T(8,128)S(1)}, f32[16,384]{1,0:T(8,128)S(1)}, u32[]{:S(2)}, u32[]{:S(2)}) %collective-permute-start.5) | collective-permute-done | bytes 24608 | tf_op jit(solution)/shard_map/ppermute | solution.py:228
  34.6 0.0 copy-done.1
  34.6 0.0 copy-done.2
  34.6 1.2 %shard_map.41 = f32[256,128]{1,0:T(8,128)} custom-call(f32[384,128]{1,0:T(8,128)S(1)} %get-tuple-element.16.both, f32[16,384]{1,0:T(8,128)S(1)} %collective-permute-done.4.low, f32[16,384]{1,0:T(8,128)S(1)} %collective-permute-done.5.high, f32[16,384]{1,0:T(8,128)S(1)} %get-tuple-element.17.up, f32[16,384]{1,0:T(8,128)S(1)} %get-tuple-element.18.down, ...), custom_call_target="tpu_custom_call" | custom-call | tf_op jit(solution)/shard_map/pallas_call | solution.py:221
  (2 shorter events, 0.0 us)
Async XLA Ops:
  0.0 5.0 %copy-start = (f32[16,16,128]{2,1,0:T(8,128)S(1)}, f32[16,16,128]{2,1,0:T(8,128)}, u32[]{:S(2)}) copy-start(f32[16,16,128]{2,1,0:T(8,128)} %field.3) | copy-start | bytes 393220
  0.0 11.6 %collective-permute-start = (f32[16,16,128]{2,1,0:T(8,128)}, f32[16,16,128]{2,1,0:T(8,128)S(1)}, u32[]{:S(2)}, u32[]{:S(2)}) collective-permute-start(f32[16,16,128]{2,1,0:T(8,128)} %field.3), channel_id=1, source_target_pairs={{0,64},{64,128},{128,192},{192,256},{256,320},{320,384},{384,448},... | collective-permute-start | bytes 393224 | tf_op jit(solution)/shard_map/ppermute | solution.py:229
  5.1 6.5 %collective-permute-start.1 = (f32[5,16,128]{2,1,0:T(8,128)S(1)}, f32[5,16,128]{2,1,0:T(8,128)S(1)}, u32[]{:S(2)}, u32[]{:S(2)}) collective-permute-start(f32[5,16,128]{2,1,0:T(8,128)S(1)} %shard_map.38), channel_id=1, source_target_pairs={{64,0},{128,64},{192,128},{256,192},{320,256},{384,320},{448,384},... | collective-permute-start | bytes 122888 | tf_op jit(solution)/shard_map/ppermute | solution.py:228
  11.7 10.5 %collective-permute-start.2 = (f32[104,128]{1,0:T(8,128)S(1)}, f32[104,128]{1,0:T(8,128)S(1)}, u32[]{:S(2)}, u32[]{:S(2)}) collective-permute-start(f32[104,128]{1,0:T(8,128)S(1)} %get-tuple-element.14), channel_id=1, source_target_pairs={{0,1},{1,2},{2,3},{3,4},{4,5},{5,6},{6,7},{8,9},{9,10},{10,11},{11... | collective-permute-start | bytes 159752 | tf_op jit(solution)/shard_map/ppermute | solution.py:229
  16.3 5.9 %collective-permute-start.3 = (f32[72,128]{1,0:T(8,128)S(1)}, f32[72,128]{1,0:T(8,128)S(1)}, u32[]{:S(2)}, u32[]{:S(2)}) collective-permute-start(f32[72,128]{1,0:T(8,128)S(1)} %get-tuple-element.15), channel_id=1, source_target_pairs={{1,0},{2,1},{3,2},{4,3},{5,4},{6,5},{7,6},{9,8},{10,9},{11,10},{12... | collective-permute-start | bytes 110600 | tf_op jit(solution)/shard_map/ppermute | solution.py:228
  22.2 12.5 %copy-start.1 = (f32[2,128,128]{2,1,0:T(8,128)S(1)}, f32[2,128,128]{2,1,0:T(8,128)}, u32[]{:S(2)}) copy-start(f32[2,128,128]{2,1,0:T(8,128)} %constant.4.clone.mains) | copy-start | bytes 393220
  22.2 12.5 %copy-start.2 = (f32[2,4,16,128]{3,2,1,0:T(8,128)S(1)}, f32[2,4,16,128]{3,2,1,0:T(8,128)}, u32[]{:S(2)}) copy-start(f32[2,4,16,128]{3,2,1,0:T(8,128)} %constant.5.clone.edges) | copy-start | bytes 196612
  22.4 6.9 %collective-permute-start.4 = (f32[16,384]{1,0:T(8,128)S(1)}, f32[16,384]{1,0:T(8,128)S(1)}, u32[]{:S(2)}, u32[]{:S(2)}) collective-permute-start(f32[16,384]{1,0:T(8,128)S(1)} %get-tuple-element.17.up), channel_id=1, source_target_pairs={{0,8},{8,16},{16,24},{24,32},{32,40},{40,48},{48,56},{1,9},{9,17},... | collective-permute-start | bytes 73736 | tf_op jit(solution)/shard_map/ppermute | solution.py:229
  27.3 7.3 %collective-permute-start.5 = (f32[16,384]{1,0:T(8,128)S(1)}, f32[16,384]{1,0:T(8,128)S(1)}, u32[]{:S(2)}, u32[]{:S(2)}) collective-permute-start(f32[16,384]{1,0:T(8,128)S(1)} %get-tuple-element.18.down), channel_id=1, source_target_pairs={{8,0},{16,8},{24,16},{32,24},{40,32},{48,40},{56,48},{9,1},{17,9},... | collective-permute-start | bytes 73736 | tf_op jit(solution)/shard_map/ppermute | solution.py:228

commit v4 on v3

--- a/solution.py
+++ b/solution.py
@@ -183,32 +183,47 @@
     down[...] = turned[:EDGE, :]
 
 
-def y_kernel(both, low, high, up, down, mains, edges, out):
+def dot(a, b):
+    return jnp.dot(a, b, precision=lax.Precision.HIGHEST, preferred_element_type=jnp.float32)
+
+
+def y_main_kernel(both, mains, out):
+    cells = BLOCK * BLOCK
+    out[:cells, :] = dot(both[:cells, :], mains[0])
+    out[cells:, :] = dot(both[cells : cells + cells // 4, :], mains[1])
+
+
+def y_kernel(main, low, high, up, down, edges, out, block, sems):
     where = lax.axis_index("gy")
     is_first, is_last = where == 0, where == lax.axis_size("gy") - 1
     cells, half = BLOCK * BLOCK, BLOCK // 2
     ends = jnp.concatenate(
         [jnp.where(is_first, down[...], low[...]), jnp.where(is_last, up[...], high[...])], axis=0
     ).T
-
-    def pass_y(k, start, stop):
-        weights = jnp.concatenate(
+    weights = [
+        jnp.concatenate(
             [jnp.where(is_first, edges[k, 1], edges[k, 0]), jnp.where(is_last, edges[k, 3], edges[k, 2])], axis=0
         )
-        return jnp.dot(
-            both[start:stop, :], mains[k], precision=lax.Precision.HIGHEST, preferred_element_type=jnp.float32
-        ) + jnp.dot(
-            ends[start:stop, :], weights, precision=lax.Precision.HIGHEST, preferred_element_type=jnp.float32
-        )
-
-    one = pass_y(0, 0, cells)
-    two = pass_y(1, cells, cells + half * half)
+        for k in range(2)
+    ]
     even = (lax.broadcasted_iota(jnp.int32, (half, LANES), 1) & 1) == 0
-    for z in range(BLOCK):
-        out[pl.ds(z, BLOCK, stride=BLOCK), :] = one[z * BLOCK : (z + 1) * BLOCK, :]
-    for z in range(half):
-        at = pl.ds(2 * z, half, stride=2 * BLOCK)
-        out[at, :] = jnp.where(even, two[z * half : (z + 1) * half, :], out[at, :])
+    whole = block.reshape(BLOCK, BLOCK, LANES)
+    copies = []
+    for part in range(2):
+        rows = slice(part * cells // 2, (part + 1) * cells // 2)
+        one = main[rows, :] + dot(ends[rows, :], weights[0])
+        rows = slice(cells + part * cells // 8, cells + (part + 1) * cells // 8)
+        two = main[rows, :] + dot(ends[rows, :], weights[1])
+        for z in range(half):
+            block[pl.ds(part * half + z, BLOCK, stride=BLOCK), :] = one[z * BLOCK : (z + 1) * BLOCK, :]
+        for z in range(half // 2):
+            at = pl.ds(part * half + 2 * z, half, stride=2 * BLOCK)
+            block[at, :] = jnp.where(even, two[z * half : (z + 1) * half, :], block[at, :])
+        span = pl.ds(part * half, half)
+        copies.append(pltpu.make_async_copy(whole.at[:, span, :], out.at[:, span, :], sems.at[part]))
+        copies[-1].start()
+    for copy in copies:
+        copy.wait()
 
 
 def near(shape):
@@ -253,18 +268,17 @@
         z_kernel, [near((wide, LANES)), near((EDGE, wide)), near((EDGE, wide))], one, two, low, high, blank
     )
     low, high = exchange(up, down, "gy")
-    (out,) = call(
+    (main,) = call(
+        y_main_kernel, [near((cells + cells // 4, LANES))], both, jnp.asarray(MAINS), flops=10**7
+    )
+    out = pl.pallas_call(
         y_kernel,
-        [jax.ShapeDtypeStruct((cells, LANES), jnp.float32)],
-        both,
-        low,
-        high,
-        up,
-        down,
-        jnp.asarray(MAINS),
-        jnp.asarray(EDGES),
-    )
-    return out.reshape(BLOCK, BLOCK, LANES)
+        out_shape=jax.ShapeDtypeStruct((BLOCK, BLOCK, LANES), jnp.float32),
+        out_specs=pl.BlockSpec(memory_space=pl.ANY),
+        scratch_shapes=[pltpu.VMEM((cells, LANES), jnp.float32), pltpu.SemaphoreType.DMA((2,))],
+        name="y_kernel",
+    )(*(pltpu.with_memory_space_constraint(a, pltpu.VMEM) for a in (main, low, high, up, down, jnp.asarray(EDGES))))
+    return out
 
 
 def solution(mesh):

time: 36.1 us -> 35.9 us (level)
  waiting for transfers between devices: 14 us -> 13.6 us
    pallas_call x0 -> x1, Pallas kernels: none -> 1.04 us  [on_device(): pl.pallas_call(y_kernel, out_shape=jax.ShapeDtypeStruct((BLOCK, BLOCK, LA...]
    pallas_call x5, Pallas kernels: 1.54 us -> 0.65 us  [call(): return pl.pallas_call(kernel, out_shape=shapes, cost_estimate=cost)(*args)]
  transfers between devices with their start and end apart: 6 -> 6, of which waited for: 3 -> 3; matrix products, arithmetic and copies ran while one was open for 0% -> 0% of each run, Pallas kernels for 0% -> 1%
where the time goes in v4:
time: 35.9 us; the launch traced here: 35.7 us
  starting transfers between devices  20.2 us (56%)
  waiting for transfers between devices  13.6 us (38%)
  Pallas kernels  1.69 us (5%)
    ppermute x3, starting transfers between devices, exchange(): low = lax.ppermute(up, axis, forward)  14.5 us
    ppermute x3, waiting for transfers between devices, exchange(): high = lax.ppermute(down, axis, backward)  13.6 us
    ppermute x3, starting transfers between devices, exchange(): high = lax.ppermute(down, axis, backward)  5.76 us
    pallas_call x1, Pallas kernels, on_device(): pl.pallas_call(y_kernel, out_shape=jax.ShapeDtypeStruct((BLOCK, BLOCK, LA...  1.04 us
  transfers between devices with their start and end apart: 6, of which 3 were waited for; matrix products, arithmetic and copies ran while one was open for 0% of the time, Pallas kernels for 1%

profile of v4, /device:TPU:311, one launch (start us, length us, event | category | flops | bytes accessed | tf_op | source)
XLA Modules:
  0.0 35.7 jit_solution(10938007018142654260)
XLA Ops:
  0.0 0.0 copy-start
  0.0 5.0 %collective-permute-start = (f32[16,16,128]{2,1,0:T(8,128)}, f32[16,16,128]{2,1,0:T(8,128)S(1)}, u32[]{:S(2)}, u32[]{:S(2)}) collective-permute-start(f32[16,16,128]{2,1,0:T(8,128)} %field.3), channel_id=1, source_target_pairs={{0,64},{64,128},{128,192},{192,256},{256,320},{320,384},{384,448},... | collective-permute-start | bytes 393224 | tf_op jit(solution)/shard_map/ppermute | solution.py:244
  5.0 0.0 copy-done
  5.1 1.9 %collective-permute-start.1 = (f32[5,16,128]{2,1,0:T(8,128)S(1)}, f32[5,16,128]{2,1,0:T(8,128)S(1)}, u32[]{:S(2)}, u32[]{:S(2)}) collective-permute-start(f32[5,16,128]{2,1,0:T(8,128)S(1)} %shard_map.38), channel_id=1, source_target_pairs={{64,0},{128,64},{192,128},{256,192},{320,256},{384,320},{448,384},... | collective-permute-start | bytes 122888 | tf_op jit(solution)/shard_map/ppermute | solution.py:243
  7.0 4.6 %collective-permute-done.1.high = f32[5,16,128]{2,1,0:T(8,128)S(1)} collective-permute-done((f32[5,16,128]{2,1,0:T(8,128)S(1)}, f32[5,16,128]{2,1,0:T(8,128)S(1)}, u32[]{:S(2)}, u32[]{:S(2)}) %collective-permute-start.1) | collective-permute-done | bytes 40992 | tf_op jit(solution)/shard_map/ppermute | solution.py:243
  11.6 0.0 collective-permute-done.low
  11.6 0.1 shard_map.39
  11.7 4.5 %collective-permute-start.2 = (f32[104,128]{1,0:T(8,128)S(1)}, f32[104,128]{1,0:T(8,128)S(1)}, u32[]{:S(2)}, u32[]{:S(2)}) collective-permute-start(f32[104,128]{1,0:T(8,128)S(1)} %get-tuple-element.14), channel_id=1, source_target_pairs={{0,1},{1,2},{2,3},{3,4},{4,5},{5,6},{6,7},{8,9},{9,10},{10,11},{11... | collective-permute-start | bytes 159752 | tf_op jit(solution)/shard_map/ppermute | solution.py:244
  16.3 1.9 %collective-permute-start.3 = (f32[72,128]{1,0:T(8,128)S(1)}, f32[72,128]{1,0:T(8,128)S(1)}, u32[]{:S(2)}, u32[]{:S(2)}) collective-permute-start(f32[72,128]{1,0:T(8,128)S(1)} %get-tuple-element.15), channel_id=1, source_target_pairs={{1,0},{2,1},{3,2},{4,3},{5,4},{6,5},{7,6},{9,8},{10,9},{11,10},{12... | collective-permute-start | bytes 110600 | tf_op jit(solution)/shard_map/ppermute | solution.py:243
  18.2 4.0 %collective-permute-done.3.high = f32[72,128]{1,0:T(8,128)S(1)} collective-permute-done((f32[72,128]{1,0:T(8,128)S(1)}, f32[72,128]{1,0:T(8,128)S(1)}, u32[]{:S(2)}, u32[]{:S(2)}) %collective-permute-start.3) | collective-permute-done | bytes 36896 | tf_op jit(solution)/shard_map/ppermute | solution.py:243
  22.2 0.0 collective-permute-done.2.low
  22.2 0.0 copy-start.1
  22.2 0.2 shard_map.40
  22.4 4.9 %collective-permute-start.4 = (f32[16,384]{1,0:T(8,128)S(1)}, f32[16,384]{1,0:T(8,128)S(1)}, u32[]{:S(2)}, u32[]{:S(2)}) collective-permute-start(f32[16,384]{1,0:T(8,128)S(1)} %get-tuple-element.17.up), channel_id=1, source_target_pairs={{0,8},{8,16},{16,24},{24,32},{32,40},{40,48},{48,56},{1,9},{9,17},... | collective-permute-start | bytes 73736 | tf_op jit(solution)/shard_map/ppermute | solution.py:244
  27.3 1.9 %collective-permute-start.5 = (f32[16,384]{1,0:T(8,128)S(1)}, f32[16,384]{1,0:T(8,128)S(1)}, u32[]{:S(2)}, u32[]{:S(2)}) collective-permute-start(f32[16,384]{1,0:T(8,128)S(1)} %get-tuple-element.18.down), channel_id=1, source_target_pairs={{8,0},{16,8},{24,16},{32,24},{40,32},{48,40},{56,48},{9,1},{17,9},... | collective-permute-start | bytes 73736 | tf_op jit(solution)/shard_map/ppermute | solution.py:243
  29.2 0.0 copy-done.1
  29.2 0.0 copy-start.2
  29.3 0.3 shard_map.41.main
  29.6 0.0 collective-permute-done.4.low
  29.6 5.1 %collective-permute-done.5.high = f32[16,384]{1,0:T(8,128)S(1)} collective-permute-done((f32[16,384]{1,0:T(8,128)S(1)}, f32[16,384]{1,0:T(8,128)S(1)}, u32[]{:S(2)}, u32[]{:S(2)}) %collective-permute-start.5) | collective-permute-done | bytes 24608 | tf_op jit(solution)/shard_map/ppermute | solution.py:243
  34.6 0.0 copy-done.2
  34.6 1.0 %y_kernel.1 = f32[16,16,128]{2,1,0:T(8,128)} custom-call(f32[320,128]{1,0:T(8,128)S(1)} %shard_map.41.main, f32[16,384]{1,0:T(8,128)S(1)} %collective-permute-done.4.low, f32[16,384]{1,0:T(8,128)S(1)} %collective-permute-done.5.high, f32[16,384]{1,0:T(8,128)S(1)} %get-tuple-element.17.up, f32[16,384]{1,0:T(8,128)S(1)} %get-tuple-element.18.down, ...), custom_call_target="tpu_custom_call" | custom-call | tf_op jit(solution)/shard_map/y_kernel/pallas_call | solution.py:274
  (2 shorter events, 0.0 us)
Async XLA Ops:
  0.0 5.0 %copy-start = (f32[16,16,128]{2,1,0:T(8,128)S(1)}, f32[16,16,128]{2,1,0:T(8,128)}, u32[]{:S(2)}) copy-start(f32[16,16,128]{2,1,0:T(8,128)} %field.3) | copy-start | bytes 393220
  0.0 11.6 %collective-permute-start = (f32[16,16,128]{2,1,0:T(8,128)}, f32[16,16,128]{2,1,0:T(8,128)S(1)}, u32[]{:S(2)}, u32[]{:S(2)}) collective-permute-start(f32[16,16,128]{2,1,0:T(8,128)} %field.3), channel_id=1, source_target_pairs={{0,64},{64,128},{128,192},{192,256},{256,320},{320,384},{384,448},... | collective-permute-start | bytes 393224 | tf_op jit(solution)/shard_map/ppermute | solution.py:244
  5.1 6.5 %collective-permute-start.1 = (f32[5,16,128]{2,1,0:T(8,128)S(1)}, f32[5,16,128]{2,1,0:T(8,128)S(1)}, u32[]{:S(2)}, u32[]{:S(2)}) collective-permute-start(f32[5,16,128]{2,1,0:T(8,128)S(1)} %shard_map.38), channel_id=1, source_target_pairs={{64,0},{128,64},{192,128},{256,192},{320,256},{384,320},{448,384},... | collective-permute-start | bytes 122888 | tf_op jit(solution)/shard_map/ppermute | solution.py:243
  11.7 10.5 %collective-permute-start.2 = (f32[104,128]{1,0:T(8,128)S(1)}, f32[104,128]{1,0:T(8,128)S(1)}, u32[]{:S(2)}, u32[]{:S(2)}) collective-permute-start(f32[104,128]{1,0:T(8,128)S(1)} %get-tuple-element.14), channel_id=1, source_target_pairs={{0,1},{1,2},{2,3},{3,4},{4,5},{5,6},{6,7},{8,9},{9,10},{10,11},{11... | collective-permute-start | bytes 159752 | tf_op jit(solution)/shard_map/ppermute | solution.py:244
  16.3 5.9 %collective-permute-start.3 = (f32[72,128]{1,0:T(8,128)S(1)}, f32[72,128]{1,0:T(8,128)S(1)}, u32[]{:S(2)}, u32[]{:S(2)}) collective-permute-start(f32[72,128]{1,0:T(8,128)S(1)} %get-tuple-element.15), channel_id=1, source_target_pairs={{1,0},{2,1},{3,2},{4,3},{5,4},{6,5},{7,6},{9,8},{10,9},{11,10},{12... | collective-permute-start | bytes 110600 | tf_op jit(solution)/shard_map/ppermute | solution.py:243
  22.2 7.1 %copy-start.1 = (f32[2,128,128]{2,1,0:T(8,128)S(1)}, f32[2,128,128]{2,1,0:T(8,128)}, u32[]{:S(2)}) copy-start(f32[2,128,128]{2,1,0:T(8,128)} %constant.4.clone.mains) | copy-start | bytes 393220
  22.4 7.2 %collective-permute-start.4 = (f32[16,384]{1,0:T(8,128)S(1)}, f32[16,384]{1,0:T(8,128)S(1)}, u32[]{:S(2)}, u32[]{:S(2)}) collective-permute-start(f32[16,384]{1,0:T(8,128)S(1)} %get-tuple-element.17.up), channel_id=1, source_target_pairs={{0,8},{8,16},{16,24},{24,32},{32,40},{40,48},{48,56},{1,9},{9,17},... | collective-permute-start | bytes 73736 | tf_op jit(solution)/shard_map/ppermute | solution.py:244
  27.3 7.3 %collective-permute-start.5 = (f32[16,384]{1,0:T(8,128)S(1)}, f32[16,384]{1,0:T(8,128)S(1)}, u32[]{:S(2)}, u32[]{:S(2)}) collective-permute-start(f32[16,384]{1,0:T(8,128)S(1)} %get-tuple-element.18.down), channel_id=1, source_target_pairs={{8,0},{16,8},{24,16},{32,24},{40,32},{48,40},{56,48},{9,1},{17,9},... | collective-permute-start | bytes 73736 | tf_op jit(solution)/shard_map/ppermute | solution.py:243
  29.2 5.4 %copy-start.2 = (f32[2,4,16,128]{3,2,1,0:T(8,128)S(1)}, f32[2,4,16,128]{3,2,1,0:T(8,128)}, u32[]{:S(2)}) copy-start(f32[2,4,16,128]{3,2,1,0:T(8,128)} %constant.5.clone.edges) | copy-start | bytes 196612

commit v5 on v4

--- a/solution.py
+++ b/solution.py
@@ -1,3 +1,5 @@
+import itertools
+
 import jax
 import jax.numpy as jnp
 import numpy as np
@@ -15,6 +17,7 @@
 BLOCK = 16
 LANES = 128
 EDGE = 16
+NEAR = {"gz": (1, 2), "gy": (2, 2)}
 
 
 STEPS = (ALPHA, BETA, GAMMA, DELTA)
@@ -131,6 +134,19 @@
 MAINS, EDGES = y_matrices()
 
 
+def swapped(axis, gx, gy, gz):
+    if axis == "gz":
+        return (gy < NEAR["gz"][0]) & (gx < NEAR["gz"][1])
+    return (gz < NEAR["gy"][0]) & (gx < NEAR["gy"][1])
+
+
+def here(axis):
+    at = {name: lax.axis_index(name) for name in ("gx", "gy", "gz")}
+    swap = swapped(axis, **at)
+    odd = lax.rem(at[axis], 2) == 1
+    return swap & odd, jnp.logical_or(jnp.logical_not(swap), odd)
+
+
 def blank_kernel(blank):
     blank[...] = jnp.zeros(blank.shape, jnp.float32)
 
@@ -141,7 +157,7 @@
         down[k] = state[key]
 
 
-def x_kernel(field, low, high, one, two, up, down):
+def x_kernel(field, low, high, one, two, send_one, send_two):
     where = lax.axis_index("gx")
     is_first, is_last = where == 0, where == lax.axis_size("gx") - 1
     half = BLOCK // 2
@@ -152,35 +168,38 @@
         one[i * BLOCK : (i + 1) * BLOCK, :] = row
     for i, row in enumerate(level_two(state, is_last)):
         two[i * BLOCK : (i + 1) * BLOCK, :] = row
-    for source, count, ups, downs in ((one, BLOCK, 3, 2), (two, half, 7, 5)):
+    up_first, _ = here("gz")
+    for source, count, base, ups, downs in ((one, BLOCK, 0, 3, 2), (two, half, 3 * BLOCK, 7, 5)):
         state = started({i: source[pl.ds(i, count, stride=BLOCK), :] for i in range(BLOCK)})
-        base = 0 if count == BLOCK else 3 * BLOCK
         for k in range(ups):
-            up[base + k * count : base + (k + 1) * count, :] = state[UP[k]]
-        base = 0 if count == BLOCK else 2 * BLOCK
-        for k in range(downs):
-            down[base + k * count : base + (k + 1) * count, :] = state[DOWN[k]]
-
-
-def z_kernel(one, two, low, high, blank, both, up, down):
+            rows = slice(base + k * count, base + (k + 1) * count)
+            up, down = state[UP[k]], state[DOWN[min(k, downs - 1)]]
+            send_one[rows, :] = jnp.where(up_first, up, down)
+            send_two[rows, :] = jnp.where(up_first, down, up)
+
+
+def z_kernel(one, two, got_one, got_two, blank, both, up, down, send_one, send_two):
     where = lax.axis_index("gz")
     is_first, is_last = where == 0, where == lax.axis_size("gz") - 1
     half = BLOCK // 2
+    _, high_first = here("gz")
     parts = []
-    for source, count, ups, downs, spans in ((one, BLOCK, 3, 2, ONE), (two, half, 7, 5, BOTH)):
+    for source, count, base, ups, downs, spans in ((one, BLOCK, 0, 3, 2, ONE), (two, half, 3 * BLOCK, 7, 5, BOTH)):
         state = started({i: source[pl.ds(i, count, stride=BLOCK), :] for i in range(BLOCK)})
-        base = 0 if count == BLOCK else 3 * BLOCK
-        lows = [low[base + k * count : base + (k + 1) * count, :] for k in range(ups)]
-        base = 0 if count == BLOCK else 2 * BLOCK
-        highs = [high[base + k * count : base + (k + 1) * count, :] for k in range(downs)]
+        rows = [slice(base + k * count, base + (k + 1) * count) for k in range(ups)]
+        lows = [jnp.where(high_first, got_two[r, :], got_one[r, :]) for r in rows]
+        highs = [jnp.where(high_first, got_one[r, :], got_two[r, :]) for r in rows[:downs]]
         joined(state, lows, highs, is_first, is_last, spans)
         parts += level_one(state) if count == BLOCK else level_two(state, is_last)
     parts.append(blank[...])
     whole = jnp.concatenate(parts, axis=0)
     both[...] = whole
     turned = whole.T
+    up_first, _ = here("gy")
     up[...] = turned[LANES - EDGE :, :]
     down[...] = turned[:EDGE, :]
+    send_one[...] = jnp.where(up_first, turned[LANES - EDGE :, :], turned[:EDGE, :])
+    send_two[...] = jnp.where(up_first, turned[:EDGE, :], turned[LANES - EDGE :, :])
 
 
 def dot(a, b):
@@ -193,13 +212,14 @@
     out[cells:, :] = dot(both[cells : cells + cells // 4, :], mains[1])
 
 
-def y_kernel(main, low, high, up, down, edges, out, block, sems):
+def y_kernel(main, got_one, got_two, up, down, edges, out, block, sems):
     where = lax.axis_index("gy")
     is_first, is_last = where == 0, where == lax.axis_size("gy") - 1
     cells, half = BLOCK * BLOCK, BLOCK // 2
-    ends = jnp.concatenate(
-        [jnp.where(is_first, down[...], low[...]), jnp.where(is_last, up[...], high[...])], axis=0
-    ).T
+    _, high_first = here("gy")
+    low = jnp.where(high_first, got_two[...], got_one[...])
+    high = jnp.where(high_first, got_one[...], got_two[...])
+    ends = jnp.concatenate([jnp.where(is_first, down[...], low), jnp.where(is_last, up[...], high)], axis=0).T
     weights = [
         jnp.concatenate(
             [jnp.where(is_first, edges[k, 1], edges[k, 0]), jnp.where(is_last, edges[k, 3], edges[k, 2])], axis=0
@@ -245,29 +265,46 @@
     return low, high
 
 
+def exchange_lines(one, two, axis):
+    names = ("gx", "gy", "gz")
+    sizes = [lax.axis_size(name) for name in names]
+    dim = names.index(axis)
+    steps = ([], [])
+    for source, at in enumerate(itertools.product(*[range(size) for size in sizes])):
+        up_first = swapped(axis, *at) and at[dim] % 2 == 1
+        for step, upward in enumerate((up_first, not up_first)):
+            to = list(at)
+            to[dim] += 1 if upward else -1
+            if 0 <= to[dim] < sizes[dim]:
+                steps[step].append((source, (to[0] * sizes[1] + to[1]) * sizes[2] + to[2]))
+    one = lax.ppermute(one, names, steps[0])
+    two = lax.ppermute(two, names, steps[1])
+    return one, two
+
+
 def on_device(field):
     cells, half = BLOCK * BLOCK, BLOCK // 2
     (blank,) = call(blank_kernel, [near((64, LANES))], flops=10**8)
     (down,) = call(x_start_kernel, [near((len(DOWN), BLOCK, LANES))], field, blank)
     low, high = exchange(field, down, "gx")
-    one, two, up, down = call(
+    one, two, send_one, send_two = call(
         x_kernel,
         [
             near((cells, LANES)),
             near((half * BLOCK, LANES)),
             near((3 * BLOCK + 7 * half, LANES)),
-            near((2 * BLOCK + 5 * half, LANES)),
+            near((3 * BLOCK + 7 * half, LANES)),
         ],
         field,
         low,
         high,
     )
-    low, high = exchange(up, down, "gz")
+    got_one, got_two = exchange_lines(send_one, send_two, "gz")
     wide = cells + 128
-    both, up, down = call(
-        z_kernel, [near((wide, LANES)), near((EDGE, wide)), near((EDGE, wide))], one, two, low, high, blank
+    both, up, down, send_one, send_two = call(
+        z_kernel, [near((wide, LANES))] + [near((EDGE, wide))] * 4, one, two, got_one, got_two, blank
     )
-    low, high = exchange(up, down, "gy")
+    got_one, got_two = exchange_lines(send_one, send_two, "gy")
     (main,) = call(
         y_main_kernel, [near((cells + cells // 4, LANES))], both, jnp.asarray(MAINS), flops=10**7
     )
@@ -277,7 +314,7 @@
         out_specs=pl.BlockSpec(memory_space=pl.ANY),
         scratch_shapes=[pltpu.VMEM((cells, LANES), jnp.float32), pltpu.SemaphoreType.DMA((2,))],
         name="y_kernel",
-    )(*(pltpu.with_memory_space_constraint(a, pltpu.VMEM) for a in (main, low, high, up, down, jnp.asarray(EDGES))))
+    )(*(pltpu.with_memory_space_constraint(a, pltpu.VMEM) for a in (main, got_one, got_two, up, down, jnp.asarray(EDGES))))
     return out
 
 

time: 35.9 us -> 30.8 us (0.86)
  the two profiles are of different devices: /device:TPU:311 before, /device:TPU:1 now
where the time goes in v5:
time: 30.8 us; the launch traced here: 30.6 us
  starting transfers between devices  22.6 us (73%)
  waiting for transfers between devices  6.09 us (20%)
  Pallas kernels  1.71 us (6%)
    ppermute x1, starting transfers between devices, exchange(): high = lax.ppermute(down, axis, backward)  12.8 us
    ppermute x2, waiting for transfers between devices, exchange_lines(): two = lax.ppermute(two, names, steps[1])  5.23 us
    ppermute x1, starting transfers between devices, exchange(): low = lax.ppermute(up, axis, forward)  4.62 us
    ppermute x2, starting transfers between devices, exchange_lines(): two = lax.ppermute(two, names, steps[1])  3.84 us
    ppermute x2, starting transfers between devices, exchange_lines(): one = lax.ppermute(one, names, steps[0])  1.33 us
    pallas_call x1, Pallas kernels, on_device(): pl.pallas_call(y_kernel, out_shape=jax.ShapeDtypeStruct((BLOCK, BLOCK, LA...  1.05 us
    ppermute x1, waiting for transfers between devices, exchange(): high = lax.ppermute(down, axis, backward)  0.85 us
    pallas_call x5, Pallas kernels, call(): return pl.pallas_call(kernel, out_shape=shapes, cost_estimate=cost)(*args)  0.66 us
  transfers between devices with their start and end apart: 6, of which 3 were waited for; matrix products, arithmetic and copies ran while one was open for 0% of the time, Pallas kernels for 1%

profile of v5, /device:TPU:1, one launch (start us, length us, event | category | flops | bytes accessed | tf_op | source)
XLA Modules:
  0.0 30.6 jit_solution(151397220438603422)
XLA Ops:
  0.0 0.0 copy-start
  0.0 4.6 %collective-permute-start = (f32[16,16,128]{2,1,0:T(8,128)}, f32[16,16,128]{2,1,0:T(8,128)S(1)}, u32[]{:S(2)}, u32[]{:S(2)}) collective-permute-start(f32[16,16,128]{2,1,0:T(8,128)} %field.3), channel_id=1, source_target_pairs={{0,64},{64,128},{128,192},{192,256},{256,320},{320,384},{384,448},... | collective-permute-start | bytes 393224 | tf_op jit(solution)/shard_map/ppermute | solution.py:264
  4.6 0.0 copy-done
  4.7 12.8 %collective-permute-start.1 = (f32[5,16,128]{2,1,0:T(8,128)S(1)}, f32[5,16,128]{2,1,0:T(8,128)S(1)}, u32[]{:S(2)}, u32[]{:S(2)}) collective-permute-start(f32[5,16,128]{2,1,0:T(8,128)S(1)} %shard_map.38), channel_id=1, source_target_pairs={{64,0},{128,64},{192,128},{256,192},{320,256},{384,320},{448,384},... | collective-permute-start | bytes 122888 | tf_op jit(solution)/shard_map/ppermute | solution.py:263
  17.5 0.8 %collective-permute-done.1.high = f32[5,16,128]{2,1,0:T(8,128)S(1)} collective-permute-done((f32[5,16,128]{2,1,0:T(8,128)S(1)}, f32[5,16,128]{2,1,0:T(8,128)S(1)}, u32[]{:S(2)}, u32[]{:S(2)}) %collective-permute-start.1) | collective-permute-done | bytes 40992 | tf_op jit(solution)/shard_map/ppermute | solution.py:263
  18.4 0.0 collective-permute-done.low
  18.4 0.1 shard_map.39
  18.5 0.7 %collective-permute-start.2 = (f32[104,128]{1,0:T(8,128)S(1)}, f32[104,128]{1,0:T(8,128)S(1)}, u32[]{:S(2)}, u32[]{:S(2)}) collective-permute-start(f32[104,128]{1,0:T(8,128)S(1)} %get-tuple-element.16), channel_id=1, source_target_pairs={{1,2},{2,1},{3,4},{4,3},{5,6},{6,5},{9,8},{10,9},{11,10},{12,11},{... | collective-permute-start | bytes 159752 | tf_op jit(solution)/shard_map/ppermute | solution.py:280
  19.2 1.9 %collective-permute-start.3 = (f32[104,128]{1,0:T(8,128)S(1)}, f32[104,128]{1,0:T(8,128)S(1)}, u32[]{:S(2)}, u32[]{:S(2)}) collective-permute-start(f32[104,128]{1,0:T(8,128)S(1)} %get-tuple-element.17), channel_id=1, source_target_pairs={{0,1},{1,0},{2,3},{3,2},{4,5},{5,4},{6,7},{7,6},{8,9},{9,10},{10,1... | collective-permute-start | bytes 159752 | tf_op jit(solution)/shard_map/ppermute | solution.py:281
  21.1 0.0 collective-permute-done.2.got_one
  21.1 2.9 %collective-permute-done.3.got_two = f32[104,128]{1,0:T(8,128)S(1)} collective-permute-done((f32[104,128]{1,0:T(8,128)S(1)}, f32[104,128]{1,0:T(8,128)S(1)}, u32[]{:S(2)}, u32[]{:S(2)}) %collective-permute-start.3) | collective-permute-done | bytes 53280 | tf_op jit(solution)/shard_map/ppermute | solution.py:281
  24.0 0.0 copy-start.1
  24.0 0.2 shard_map.40
  24.2 0.7 %collective-permute-start.4 = (f32[16,384]{1,0:T(8,128)S(1)}, f32[16,384]{1,0:T(8,128)S(1)}, u32[]{:S(2)}, u32[]{:S(2)}) collective-permute-start(f32[16,384]{1,0:T(8,128)S(1)} %get-tuple-element.19), channel_id=1, source_target_pairs={{8,16},{9,17},{10,2},{11,3},{12,4},{13,5},{14,6},{15,7},{16,8},{17... | collective-permute-start | bytes 73736 | tf_op jit(solution)/shard_map/ppermute | solution.py:280
  24.9 1.9 %collective-permute-start.5 = (f32[16,384]{1,0:T(8,128)S(1)}, f32[16,384]{1,0:T(8,128)S(1)}, u32[]{:S(2)}, u32[]{:S(2)}) collective-permute-start(f32[16,384]{1,0:T(8,128)S(1)} %get-tuple-element.20), channel_id=1, source_target_pairs={{0,8},{1,9},{2,10},{3,11},{4,12},{5,13},{6,14},{7,15},{8,0},{9,1},... | collective-permute-start | bytes 73736 | tf_op jit(solution)/shard_map/ppermute | solution.py:281
  26.9 0.0 copy-done.1
  26.9 0.0 copy-start.2
  26.9 0.3 %shard_map.41.main = f32[320,128]{1,0:T(8,128)S(1)} custom-call(f32[384,128]{1,0:T(8,128)S(1)} %get-tuple-element.18.both, f32[2,128,128]{2,1,0:T(8,128)S(1)} %copy-done.1), custom_call_target="tpu_custom_call" | custom-call | flops 10000000 | bytes 4096 | tf_op jit(solution)/shard_map/pallas_call | solution.py:256
  27.2 0.0 collective-permute-done.4.got_one
  27.2 2.3 %collective-permute-done.5.got_two = f32[16,384]{1,0:T(8,128)S(1)} collective-permute-done((f32[16,384]{1,0:T(8,128)S(1)}, f32[16,384]{1,0:T(8,128)S(1)}, u32[]{:S(2)}, u32[]{:S(2)}) %collective-permute-start.5) | collective-permute-done | bytes 24608 | tf_op jit(solution)/shard_map/ppermute | solution.py:281
  29.5 0.0 copy-done.2
  29.5 1.1 %y_kernel.1 = f32[16,16,128]{2,1,0:T(8,128)} custom-call(f32[320,128]{1,0:T(8,128)S(1)} %shard_map.41.main, f32[16,384]{1,0:T(8,128)S(1)} %collective-permute-done.4.got_one, f32[16,384]{1,0:T(8,128)S(1)} %collective-permute-done.5.got_two, f32[16,384]{1,0:T(8,128)S(1)} %get-tuple-element.21.up, f32[16,384]{1,0:T(8,128)S(1)} %get-tuple-element.22.down, ...), custom_call_target="tpu_custom_call" | custom-call | tf_op jit(solution)/shard_map/y_kernel/pallas_call | solution.py:311
  (2 shorter events, 0.0 us)
Async XLA Ops:
  0.0 4.6 %copy-start = (f32[16,16,128]{2,1,0:T(8,128)S(1)}, f32[16,16,128]{2,1,0:T(8,128)}, u32[]{:S(2)}) copy-start(f32[16,16,128]{2,1,0:T(8,128)} %field.3) | copy-start | bytes 393220
  0.0 18.4 %collective-permute-start = (f32[16,16,128]{2,1,0:T(8,128)}, f32[16,16,128]{2,1,0:T(8,128)S(1)}, u32[]{:S(2)}, u32[]{:S(2)}) collective-permute-start(f32[16,16,128]{2,1,0:T(8,128)} %field.3), channel_id=1, source_target_pairs={{0,64},{64,128},{128,192},{192,256},{256,320},{320,384},{384,448},... | collective-permute-start | bytes 393224 | tf_op jit(solution)/shard_map/ppermute | solution.py:264
  4.7 13.7 %collective-permute-start.1 = (f32[5,16,128]{2,1,0:T(8,128)S(1)}, f32[5,16,128]{2,1,0:T(8,128)S(1)}, u32[]{:S(2)}, u32[]{:S(2)}) collective-permute-start(f32[5,16,128]{2,1,0:T(8,128)S(1)} %shard_map.38), channel_id=1, source_target_pairs={{64,0},{128,64},{192,128},{256,192},{320,256},{384,320},{448,384},... | collective-permute-start | bytes 122888 | tf_op jit(solution)/shard_map/ppermute | solution.py:263
  18.5 2.6 %collective-permute-start.2 = (f32[104,128]{1,0:T(8,128)S(1)}, f32[104,128]{1,0:T(8,128)S(1)}, u32[]{:S(2)}, u32[]{:S(2)}) collective-permute-start(f32[104,128]{1,0:T(8,128)S(1)} %get-tuple-element.16), channel_id=1, source_target_pairs={{1,2},{2,1},{3,4},{4,3},{5,6},{6,5},{9,8},{10,9},{11,10},{12,11},{... | collective-permute-start | bytes 159752 | tf_op jit(solution)/shard_map/ppermute | solution.py:280
  19.2 4.9 %collective-permute-start.3 = (f32[104,128]{1,0:T(8,128)S(1)}, f32[104,128]{1,0:T(8,128)S(1)}, u32[]{:S(2)}, u32[]{:S(2)}) collective-permute-start(f32[104,128]{1,0:T(8,128)S(1)} %get-tuple-element.17), channel_id=1, source_target_pairs={{0,1},{1,0},{2,3},{3,2},{4,5},{5,4},{6,7},{7,6},{8,9},{9,10},{10,1... | collective-permute-start | bytes 159752 | tf_op jit(solution)/shard_map/ppermute | solution.py:281
  24.0 2.8 %copy-start.1 = (f32[2,128,128]{2,1,0:T(8,128)S(1)}, f32[2,128,128]{2,1,0:T(8,128)}, u32[]{:S(2)}) copy-start(f32[2,128,128]{2,1,0:T(8,128)} %constant.4.clone.mains) | copy-start | bytes 393220
  24.2 2.9 %collective-permute-start.4 = (f32[16,384]{1,0:T(8,128)S(1)}, f32[16,384]{1,0:T(8,128)S(1)}, u32[]{:S(2)}, u32[]{:S(2)}) collective-permute-start(f32[16,384]{1,0:T(8,128)S(1)} %get-tuple-element.19), channel_id=1, source_target_pairs={{8,16},{9,17},{10,2},{11,3},{12,4},{13,5},{14,6},{15,7},{16,8},{17... | collective-permute-start | bytes 73736 | tf_op jit(solution)/shard_map/ppermute | solution.py:280
  24.9 4.6 %collective-permute-start.5 = (f32[16,384]{1,0:T(8,128)S(1)}, f32[16,384]{1,0:T(8,128)S(1)}, u32[]{:S(2)}, u32[]{:S(2)}) collective-permute-start(f32[16,384]{1,0:T(8,128)S(1)} %get-tuple-element.20), channel_id=1, source_target_pairs={{0,8},{1,9},{2,10},{3,11},{4,12},{5,13},{6,14},{7,15},{8,0},{9,1},... | collective-permute-start | bytes 73736 | tf_op jit(solution)/shard_map/ppermute | solution.py:281
  26.9 2.6 %copy-start.2 = (f32[2,4,16,128]{3,2,1,0:T(8,128)S(1)}, f32[2,4,16,128]{3,2,1,0:T(8,128)}, u32[]{:S(2)}) copy-start(f32[2,4,16,128]{3,2,1,0:T(8,128)} %constant.5.clone.edges) | copy-start | bytes 196612

commit v6 on v5

--- a/solution.py
+++ b/solution.py
@@ -17,7 +17,7 @@
 BLOCK = 16
 LANES = 128
 EDGE = 16
-NEAR = {"gz": (1, 2), "gy": (2, 2)}
+NEAR = {"gx": (1, 1), "gz": (1, 2), "gy": (2, 2)}
 
 
 STEPS = (ALPHA, BETA, GAMMA, DELTA)
@@ -135,6 +135,8 @@
 
 
 def swapped(axis, gx, gy, gz):
+    if axis == "gx":
+        return (gy < NEAR["gx"][0]) & (gz < NEAR["gx"][1])
     if axis == "gz":
         return (gy < NEAR["gz"][0]) & (gx < NEAR["gz"][1])
     return (gz < NEAR["gy"][0]) & (gx < NEAR["gy"][1])
@@ -151,19 +153,25 @@
     blank[...] = jnp.zeros(blank.shape, jnp.float32)
 
 
-def x_start_kernel(field, blank, down):
+def x_start_kernel(field, blank, send_two):
     state = started({i: field[i] for i in range(BLOCK)})
-    for k, key in enumerate(DOWN):
-        down[k] = state[key]
-
-
-def x_kernel(field, low, high, one, two, send_one, send_two):
+    up_first, _ = here("gx")
+    swap = swapped("gx", *(lax.axis_index(name) for name in ("gx", "gy", "gz")))
+    goes_up = swap & jnp.logical_not(up_first)
+    for k, key in enumerate(UP):
+        send_two[k] = jnp.where(goes_up, state[key], state[DOWN[min(k, len(DOWN) - 1)]])
+
+
+def x_kernel(field, got_one, got_two, one, two, send_one, send_two):
     where = lax.axis_index("gx")
     is_first, is_last = where == 0, where == lax.axis_size("gx") - 1
     half = BLOCK // 2
-    before = started({i: low[i] for i in range(BLOCK)})
+    up_first, _ = here("gx")
+    beside = started({i: got_one[i] for i in range(BLOCK)})
     state = started({i: field[i] for i in range(BLOCK)})
-    joined(state, [before[key] for key in UP], [high[k] for k in range(len(DOWN))], is_first, is_last, BOTH)
+    lows = [jnp.where(up_first, got_two[k], beside[key]) for k, key in enumerate(UP)]
+    highs = [jnp.where(up_first, beside[key], got_two[k]) for k, key in enumerate(DOWN)]
+    joined(state, lows, highs, is_first, is_last, BOTH)
     for i, row in enumerate(level_one(state)):
         one[i * BLOCK : (i + 1) * BLOCK, :] = row
     for i, row in enumerate(level_two(state, is_last)):
@@ -256,22 +264,16 @@
     return pl.pallas_call(kernel, out_shape=shapes, cost_estimate=cost)(*args)
 
 
-def exchange(up, down, axis):
-    count = lax.axis_size(axis)
-    forward = [(i, i + 1) for i in range(count - 1)]
-    backward = [(target, source) for source, target in forward]
-    high = lax.ppermute(down, axis, backward)
-    low = lax.ppermute(up, axis, forward)
-    return low, high
-
-
 def exchange_lines(one, two, axis):
     names = ("gx", "gy", "gz")
     sizes = [lax.axis_size(name) for name in names]
     dim = names.index(axis)
     steps = ([], [])
     for source, at in enumerate(itertools.product(*[range(size) for size in sizes])):
-        up_first = swapped(axis, *at) and at[dim] % 2 == 1
+        if swapped(axis, *at):
+            up_first = at[dim] % 2 == 1
+        else:
+            up_first = axis == "gx"
         for step, upward in enumerate((up_first, not up_first)):
             to = list(at)
             to[dim] += 1 if upward else -1
@@ -285,8 +287,8 @@
 def on_device(field):
     cells, half = BLOCK * BLOCK, BLOCK // 2
     (blank,) = call(blank_kernel, [near((64, LANES))], flops=10**8)
-    (down,) = call(x_start_kernel, [near((len(DOWN), BLOCK, LANES))], field, blank)
-    low, high = exchange(field, down, "gx")
+    (send_two,) = call(x_start_kernel, [near((len(UP), BLOCK, LANES))], field, blank)
+    got_one, got_two = exchange_lines(field, send_two, "gx")
     one, two, send_one, send_two = call(
         x_kernel,
         [
@@ -296,8 +298,8 @@
             near((3 * BLOCK + 7 * half, LANES)),
         ],
         field,
-        low,
-        high,
+        got_one,
+        got_two,
     )
     got_one, got_two = exchange_lines(send_one, send_two, "gz")
     wide = cells + 128

time: 30.8 us -> 30.5 us (level)
  the two profiles are of different devices: /device:TPU:1 before, /device:TPU:455 now
where the time goes in v6:
time: 30.5 us; the launch traced here: 30.2 us
  starting transfers between devices  20.3 us (67%)
  waiting for transfers between devices  8.11 us (27%)
  Pallas kernels  1.72 us (6%)
    ppermute x3, starting transfers between devices, exchange_lines(): two = lax.ppermute(two, names, steps[1])  11.4 us
    ppermute x3, starting transfers between devices, exchange_lines(): one = lax.ppermute(one, names, steps[0])  8.89 us
    ppermute x3, waiting for transfers between devices, exchange_lines(): two = lax.ppermute(two, names, steps[1])  8.1 us
    pallas_call x1, Pallas kernels, on_device(): pl.pallas_call(y_kernel, out_shape=jax.ShapeDtypeStruct((BLOCK, BLOCK, LA...  1.05 us
    pallas_call x5, Pallas kernels, call(): return pl.pallas_call(kernel, out_shape=shapes, cost_estimate=cost)(*args)  0.67 us
  transfers between devices with their start and end apart: 6, of which 3 were waited for; matrix products, arithmetic and copies ran while one was open for 0% of the time, Pallas kernels for 1%

profile of v6, /device:TPU:455, one launch (start us, length us, event | category | flops | bytes accessed | tf_op | source)
XLA Modules:
  0.0 30.2 jit_solution(9906869192210153175)
XLA Ops:
  0.0 0.0 copy-start
  0.0 5.0 %collective-permute-start = (f32[16,16,128]{2,1,0:T(8,128)}, f32[16,16,128]{2,1,0:T(8,128)S(1)}, u32[]{:S(2)}, u32[]{:S(2)}) collective-permute-start(f32[16,16,128]{2,1,0:T(8,128)} %field.3), channel_id=1, source_target_pairs={{1,65},{2,66},{3,67},{4,68},{5,69},{6,70},{7,71},{8,72},{9,73},{10... | collective-permute-start | bytes 393224 | tf_op jit(solution)/shard_map/ppermute | solution.py:282
  5.0 0.0 copy-done
  5.1 1.9 %collective-permute-start.1 = (f32[7,16,128]{2,1,0:T(8,128)S(1)}, f32[7,16,128]{2,1,0:T(8,128)S(1)}, u32[]{:S(2)}, u32[]{:S(2)}) collective-permute-start(f32[7,16,128]{2,1,0:T(8,128)S(1)} %shard_map.38), channel_id=1, source_target_pairs={{0,64},{64,0},{65,1},{66,2},{67,3},{68,4},{69,5},{70,6},{71,7},{72... | collective-permute-start | bytes 172040 | tf_op jit(solution)/shard_map/ppermute | solution.py:283
  7.0 4.8 %collective-permute-done.1.got_two = f32[7,16,128]{2,1,0:T(8,128)S(1)} collective-permute-done((f32[7,16,128]{2,1,0:T(8,128)S(1)}, f32[7,16,128]{2,1,0:T(8,128)S(1)}, u32[]{:S(2)}, u32[]{:S(2)}) %collective-permute-start.1) | collective-permute-done | bytes 57376 | tf_op jit(solution)/shard_map/ppermute | solution.py:283
  11.8 0.0 collective-permute-done.got_one
  11.8 0.1 shard_map.39
  11.9 2.0 %collective-permute-start.2 = (f32[104,128]{1,0:T(8,128)S(1)}, f32[104,128]{1,0:T(8,128)S(1)}, u32[]{:S(2)}, u32[]{:S(2)}) collective-permute-start(f32[104,128]{1,0:T(8,128)S(1)} %get-tuple-element.16), channel_id=1, source_target_pairs={{1,2},{2,1},{3,4},{4,3},{5,6},{6,5},{9,8},{10,9},{11,10},{12,11},{... | collective-permute-start | bytes 159752 | tf_op jit(solution)/shard_map/ppermute | solution.py:282
  13.9 3.3 %collective-permute-start.3 = (f32[104,128]{1,0:T(8,128)S(1)}, f32[104,128]{1,0:T(8,128)S(1)}, u32[]{:S(2)}, u32[]{:S(2)}) collective-permute-start(f32[104,128]{1,0:T(8,128)S(1)} %get-tuple-element.17), channel_id=1, source_target_pairs={{0,1},{1,0},{2,3},{3,2},{4,5},{5,4},{6,7},{7,6},{8,9},{9,10},{10,1... | collective-permute-start | bytes 159752 | tf_op jit(solution)/shard_map/ppermute | solution.py:283
  17.2 0.0 collective-permute-done.2.got_one
  17.2 2.7 %collective-permute-done.3.got_two = f32[104,128]{1,0:T(8,128)S(1)} collective-permute-done((f32[104,128]{1,0:T(8,128)S(1)}, f32[104,128]{1,0:T(8,128)S(1)}, u32[]{:S(2)}, u32[]{:S(2)}) %collective-permute-start.3) | collective-permute-done | bytes 53280 | tf_op jit(solution)/shard_map/ppermute | solution.py:283
  20.0 0.0 copy-start.1
  20.0 0.2 shard_map.40
  20.2 1.9 %collective-permute-start.4 = (f32[16,384]{1,0:T(8,128)S(1)}, f32[16,384]{1,0:T(8,128)S(1)}, u32[]{:S(2)}, u32[]{:S(2)}) collective-permute-start(f32[16,384]{1,0:T(8,128)S(1)} %get-tuple-element.19), channel_id=1, source_target_pairs={{8,16},{9,17},{10,2},{11,3},{12,4},{13,5},{14,6},{15,7},{16,8},{17... | collective-permute-start | bytes 73736 | tf_op jit(solution)/shard_map/ppermute | solution.py:282
  22.1 6.1 %collective-permute-start.5 = (f32[16,384]{1,0:T(8,128)S(1)}, f32[16,384]{1,0:T(8,128)S(1)}, u32[]{:S(2)}, u32[]{:S(2)}) collective-permute-start(f32[16,384]{1,0:T(8,128)S(1)} %get-tuple-element.20), channel_id=1, source_target_pairs={{0,8},{1,9},{2,10},{3,11},{4,12},{5,13},{6,14},{7,15},{8,0},{9,1},... | collective-permute-start | bytes 73736 | tf_op jit(solution)/shard_map/ppermute | solution.py:283
  28.3 0.0 copy-done.1
  28.3 0.0 copy-start.2
  28.3 0.3 %shard_map.41.main = f32[320,128]{1,0:T(8,128)S(1)} custom-call(f32[384,128]{1,0:T(8,128)S(1)} %get-tuple-element.18.both, f32[2,128,128]{2,1,0:T(8,128)S(1)} %copy-done.1), custom_call_target="tpu_custom_call" | custom-call | flops 10000000 | bytes 4096 | tf_op jit(solution)/shard_map/pallas_call | solution.py:264
  28.6 0.0 collective-permute-done.4.got_one
  28.6 0.6 %collective-permute-done.5.got_two = f32[16,384]{1,0:T(8,128)S(1)} collective-permute-done((f32[16,384]{1,0:T(8,128)S(1)}, f32[16,384]{1,0:T(8,128)S(1)}, u32[]{:S(2)}, u32[]{:S(2)}) %collective-permute-start.5) | collective-permute-done | bytes 24608 | tf_op jit(solution)/shard_map/ppermute | solution.py:283
  29.2 0.0 copy-done.2
  29.2 1.0 %y_kernel.1 = f32[16,16,128]{2,1,0:T(8,128)} custom-call(f32[320,128]{1,0:T(8,128)S(1)} %shard_map.41.main, f32[16,384]{1,0:T(8,128)S(1)} %collective-permute-done.4.got_one, f32[16,384]{1,0:T(8,128)S(1)} %collective-permute-done.5.got_two, f32[16,384]{1,0:T(8,128)S(1)} %get-tuple-element.21.up, f32[16,384]{1,0:T(8,128)S(1)} %get-tuple-element.22.down, ...), custom_call_target="tpu_custom_call" | custom-call | tf_op jit(solution)/shard_map/y_kernel/pallas_call | solution.py:313
  (2 shorter events, 0.0 us)
Async XLA Ops:
  0.0 5.0 %copy-start = (f32[16,16,128]{2,1,0:T(8,128)S(1)}, f32[16,16,128]{2,1,0:T(8,128)}, u32[]{:S(2)}) copy-start(f32[16,16,128]{2,1,0:T(8,128)} %field.3) | copy-start | bytes 393220
  0.0 11.8 %collective-permute-start = (f32[16,16,128]{2,1,0:T(8,128)}, f32[16,16,128]{2,1,0:T(8,128)S(1)}, u32[]{:S(2)}, u32[]{:S(2)}) collective-permute-start(f32[16,16,128]{2,1,0:T(8,128)} %field.3), channel_id=1, source_target_pairs={{1,65},{2,66},{3,67},{4,68},{5,69},{6,70},{7,71},{8,72},{9,73},{10... | collective-permute-start | bytes 393224 | tf_op jit(solution)/shard_map/ppermute | solution.py:282
  5.1 6.7 %collective-permute-start.1 = (f32[7,16,128]{2,1,0:T(8,128)S(1)}, f32[7,16,128]{2,1,0:T(8,128)S(1)}, u32[]{:S(2)}, u32[]{:S(2)}) collective-permute-start(f32[7,16,128]{2,1,0:T(8,128)S(1)} %shard_map.38), channel_id=1, source_target_pairs={{0,64},{64,0},{65,1},{66,2},{67,3},{68,4},{69,5},{70,6},{71,7},{72... | collective-permute-start | bytes 172040 | tf_op jit(solution)/shard_map/ppermute | solution.py:283
  11.9 5.3 %collective-permute-start.2 = (f32[104,128]{1,0:T(8,128)S(1)}, f32[104,128]{1,0:T(8,128)S(1)}, u32[]{:S(2)}, u32[]{:S(2)}) collective-permute-start(f32[104,128]{1,0:T(8,128)S(1)} %get-tuple-element.16), channel_id=1, source_target_pairs={{1,2},{2,1},{3,4},{4,3},{5,6},{6,5},{9,8},{10,9},{11,10},{12,11},{... | collective-permute-start | bytes 159752 | tf_op jit(solution)/shard_map/ppermute | solution.py:282
  13.9 6.1 %collective-permute-start.3 = (f32[104,128]{1,0:T(8,128)S(1)}, f32[104,128]{1,0:T(8,128)S(1)}, u32[]{:S(2)}, u32[]{:S(2)}) collective-permute-start(f32[104,128]{1,0:T(8,128)S(1)} %get-tuple-element.17), channel_id=1, source_target_pairs={{0,1},{1,0},{2,3},{3,2},{4,5},{5,4},{6,7},{7,6},{8,9},{9,10},{10,1... | collective-permute-start | bytes 159752 | tf_op jit(solution)/shard_map/ppermute | solution.py:283
  20.0 8.3 %copy-start.1 = (f32[2,128,128]{2,1,0:T(8,128)S(1)}, f32[2,128,128]{2,1,0:T(8,128)}, u32[]{:S(2)}) copy-start(f32[2,128,128]{2,1,0:T(8,128)} %constant.4.clone.mains) | copy-start | bytes 393220
  20.2 8.4 %collective-permute-start.4 = (f32[16,384]{1,0:T(8,128)S(1)}, f32[16,384]{1,0:T(8,128)S(1)}, u32[]{:S(2)}, u32[]{:S(2)}) collective-permute-start(f32[16,384]{1,0:T(8,128)S(1)} %get-tuple-element.19), channel_id=1, source_target_pairs={{8,16},{9,17},{10,2},{11,3},{12,4},{13,5},{14,6},{15,7},{16,8},{17... | collective-permute-start | bytes 73736 | tf_op jit(solution)/shard_map/ppermute | solution.py:282
  22.1 7.1 %collective-permute-start.5 = (f32[16,384]{1,0:T(8,128)S(1)}, f32[16,384]{1,0:T(8,128)S(1)}, u32[]{:S(2)}, u32[]{:S(2)}) collective-permute-start(f32[16,384]{1,0:T(8,128)S(1)} %get-tuple-element.20), channel_id=1, source_target_pairs={{0,8},{1,9},{2,10},{3,11},{4,12},{5,13},{6,14},{7,15},{8,0},{9,1},... | collective-permute-start | bytes 73736 | tf_op jit(solution)/shard_map/ppermute | solution.py:283
  28.3 0.9 %copy-start.2 = (f32[2,4,16,128]{3,2,1,0:T(8,128)S(1)}, f32[2,4,16,128]{3,2,1,0:T(8,128)}, u32[]{:S(2)}) copy-start(f32[2,4,16,128]{3,2,1,0:T(8,128)} %constant.5.clone.edges) | copy-start | bytes 196612

commit v7 on v6

--- a/solution.py
+++ b/solution.py
@@ -17,7 +17,7 @@
 BLOCK = 16
 LANES = 128
 EDGE = 16
-NEAR = {"gx": (1, 1), "gz": (1, 2), "gy": (2, 2)}
+NEAR = {"gx": (8, 8), "gz": (1, 2), "gy": 2}
 
 
 STEPS = (ALPHA, BETA, GAMMA, DELTA)
@@ -139,7 +139,7 @@
         return (gy < NEAR["gx"][0]) & (gz < NEAR["gx"][1])
     if axis == "gz":
         return (gy < NEAR["gz"][0]) & (gx < NEAR["gz"][1])
-    return (gz < NEAR["gy"][0]) & (gx < NEAR["gy"][1])
+    return gz + gx < NEAR["gy"]
 
 
 def here(axis):
@@ -214,6 +214,17 @@
     return jnp.dot(a, b, precision=lax.Precision.HIGHEST, preferred_element_type=jnp.float32)
 
 
+def split(v):
+    high = v.astype(jnp.bfloat16)
+    rest = v - high.astype(jnp.float32)
+    middle = rest.astype(jnp.bfloat16)
+    return high, middle, (rest - middle.astype(jnp.float32)).astype(jnp.bfloat16)
+
+
+def turned_dot(a, b):
+    return lax.dot_general(a, b, (((0,), (0,)), ((), ())), preferred_element_type=jnp.float32)
+
+
 def y_main_kernel(both, mains, out):
     cells = BLOCK * BLOCK
     out[:cells, :] = dot(both[:cells, :], mains[0])
@@ -227,21 +238,25 @@
     _, high_first = here("gy")
     low = jnp.where(high_first, got_two[...], got_one[...])
     high = jnp.where(high_first, got_one[...], got_two[...])
-    ends = jnp.concatenate([jnp.where(is_first, down[...], low), jnp.where(is_last, up[...], high)], axis=0).T
-    weights = [
-        jnp.concatenate(
-            [jnp.where(is_first, edges[k, 1], edges[k, 0]), jnp.where(is_last, edges[k, 3], edges[k, 2])], axis=0
+    ends = jnp.concatenate([jnp.where(is_first, down[...], low), jnp.where(is_last, up[...], high)], axis=0)
+    big, mid, small = split(ends)
+    ends = jnp.concatenate([big, big, mid, mid, big, small], axis=0)
+    weights = []
+    for k in range(2):
+        big, mid, small = split(
+            jnp.concatenate(
+                [jnp.where(is_first, edges[k, 1], edges[k, 0]), jnp.where(is_last, edges[k, 3], edges[k, 2])], axis=0
+            )
         )
-        for k in range(2)
-    ]
+        weights.append(jnp.concatenate([big, mid, big, mid, small, big], axis=0))
+    coarse = main[cells:, :] + turned_dot(ends[:, cells:], weights[1])[: cells // 4, :]
     even = (lax.broadcasted_iota(jnp.int32, (half, LANES), 1) & 1) == 0
     whole = block.reshape(BLOCK, BLOCK, LANES)
     copies = []
     for part in range(2):
         rows = slice(part * cells // 2, (part + 1) * cells // 2)
-        one = main[rows, :] + dot(ends[rows, :], weights[0])
-        rows = slice(cells + part * cells // 8, cells + (part + 1) * cells // 8)
-        two = main[rows, :] + dot(ends[rows, :], weights[1])
+        one = main[rows, :] + turned_dot(ends[:, rows], weights[0])
+        two = coarse[part * cells // 8 : (part + 1) * cells // 8, :]
         for z in range(half):
             block[pl.ds(part * half + z, BLOCK, stride=BLOCK), :] = one[z * BLOCK : (z + 1) * BLOCK, :]
         for z in range(half // 2):

time: 30.5 us -> 30.2 us (level)
  the two profiles are of different devices: /device:TPU:455 before, /device:TPU:1 now
where the time goes in v7:
time: 30.2 us; the launch traced here: 29.9 us
  starting transfers between devices  22.1 us (73%)
  waiting for transfers between devices  6.11 us (20%)
  Pallas kernels  1.62 us (5%)
    ppermute x3, starting transfers between devices, exchange_lines(): two = lax.ppermute(two, names, steps[1])  16.1 us
    ppermute x3, waiting for transfers between devices, exchange_lines(): two = lax.ppermute(two, names, steps[1])  6.1 us
    ppermute x3, starting transfers between devices, exchange_lines(): one = lax.ppermute(one, names, steps[0])  5.95 us
    pallas_call x1, Pallas kernels, on_device(): pl.pallas_call(y_kernel, out_shape=jax.ShapeDtypeStruct((BLOCK, BLOCK, LA...  0.95 us
    pallas_call x5, Pallas kernels, call(): return pl.pallas_call(kernel, out_shape=shapes, cost_estimate=cost)(*args)  0.67 us
  transfers between devices with their start and end apart: 6, of which 3 were waited for; matrix products, arithmetic and copies ran while one was open for 0% of the time, Pallas kernels for 1%

profile of v7, /device:TPU:1, one launch (start us, length us, event | category | flops | bytes accessed | tf_op | source)
XLA Modules:
  0.0 29.9 jit_solution(14086097910689137558)
XLA Ops:
  0.0 0.0 copy-start
  0.0 4.6 %collective-permute-start = (f32[16,16,128]{2,1,0:T(8,128)}, f32[16,16,128]{2,1,0:T(8,128)S(1)}, u32[]{:S(2)}, u32[]{:S(2)}) collective-permute-start(f32[16,16,128]{2,1,0:T(8,128)} %field.3), channel_id=1, source_target_pairs={{64,128},{65,129},{66,130},{67,131},{68,132},{69,133},{70,134},{71... | collective-permute-start | bytes 393224 | tf_op jit(solution)/shard_map/ppermute | solution.py:297
  4.6 0.0 copy-done
  4.7 12.3 %collective-permute-start.1 = (f32[7,16,128]{2,1,0:T(8,128)S(1)}, f32[7,16,128]{2,1,0:T(8,128)S(1)}, u32[]{:S(2)}, u32[]{:S(2)}) collective-permute-start(f32[7,16,128]{2,1,0:T(8,128)S(1)} %shard_map.38), channel_id=1, source_target_pairs={{0,64},{1,65},{2,66},{3,67},{4,68},{5,69},{6,70},{7,71},{8,72},{9,... | collective-permute-start | bytes 172040 | tf_op jit(solution)/shard_map/ppermute | solution.py:298
  17.0 0.9 %collective-permute-done.1.got_two = f32[7,16,128]{2,1,0:T(8,128)S(1)} collective-permute-done((f32[7,16,128]{2,1,0:T(8,128)S(1)}, f32[7,16,128]{2,1,0:T(8,128)S(1)}, u32[]{:S(2)}, u32[]{:S(2)}) %collective-permute-start.1) | collective-permute-done | bytes 57376 | tf_op jit(solution)/shard_map/ppermute | solution.py:298
  17.8 0.0 collective-permute-done.got_one
  17.8 0.1 shard_map.39
  18.0 0.7 %collective-permute-start.2 = (f32[104,128]{1,0:T(8,128)S(1)}, f32[104,128]{1,0:T(8,128)S(1)}, u32[]{:S(2)}, u32[]{:S(2)}) collective-permute-start(f32[104,128]{1,0:T(8,128)S(1)} %get-tuple-element.16), channel_id=1, source_target_pairs={{1,2},{2,1},{3,4},{4,3},{5,6},{6,5},{9,8},{10,9},{11,10},{12,11},{... | collective-permute-start | bytes 159752 | tf_op jit(solution)/shard_map/ppermute | solution.py:297
  18.6 1.9 %collective-permute-start.3 = (f32[104,128]{1,0:T(8,128)S(1)}, f32[104,128]{1,0:T(8,128)S(1)}, u32[]{:S(2)}, u32[]{:S(2)}) collective-permute-start(f32[104,128]{1,0:T(8,128)S(1)} %get-tuple-element.17), channel_id=1, source_target_pairs={{0,1},{1,0},{2,3},{3,2},{4,5},{5,4},{6,7},{7,6},{8,9},{9,10},{10,1... | collective-permute-start | bytes 159752 | tf_op jit(solution)/shard_map/ppermute | solution.py:298
  20.6 0.0 collective-permute-done.2.got_one
  20.6 2.9 %collective-permute-done.3.got_two = f32[104,128]{1,0:T(8,128)S(1)} collective-permute-done((f32[104,128]{1,0:T(8,128)S(1)}, f32[104,128]{1,0:T(8,128)S(1)}, u32[]{:S(2)}, u32[]{:S(2)}) %collective-permute-start.3) | collective-permute-done | bytes 53280 | tf_op jit(solution)/shard_map/ppermute | solution.py:298
  23.5 0.0 copy-start.1
  23.5 0.2 shard_map.40
  23.7 0.7 %collective-permute-start.4 = (f32[16,384]{1,0:T(8,128)S(1)}, f32[16,384]{1,0:T(8,128)S(1)}, u32[]{:S(2)}, u32[]{:S(2)}) collective-permute-start(f32[16,384]{1,0:T(8,128)S(1)} %get-tuple-element.19), channel_id=1, source_target_pairs={{8,16},{9,17},{10,2},{11,3},{12,4},{13,5},{14,6},{15,7},{16,8},{17... | collective-permute-start | bytes 73736 | tf_op jit(solution)/shard_map/ppermute | solution.py:297
  24.4 1.9 %collective-permute-start.5 = (f32[16,384]{1,0:T(8,128)S(1)}, f32[16,384]{1,0:T(8,128)S(1)}, u32[]{:S(2)}, u32[]{:S(2)}) collective-permute-start(f32[16,384]{1,0:T(8,128)S(1)} %get-tuple-element.20), channel_id=1, source_target_pairs={{0,8},{1,9},{2,10},{3,11},{4,12},{5,13},{6,14},{7,15},{8,0},{9,1},... | collective-permute-start | bytes 73736 | tf_op jit(solution)/shard_map/ppermute | solution.py:298
  26.3 0.0 copy-done.1
  26.3 0.0 copy-start.2
  26.4 0.3 %shard_map.41.main = f32[320,128]{1,0:T(8,128)S(1)} custom-call(f32[384,128]{1,0:T(8,128)S(1)} %get-tuple-element.18.both, f32[2,128,128]{2,1,0:T(8,128)S(1)} %copy-done.1), custom_call_target="tpu_custom_call" | custom-call | flops 10000000 | bytes 4096 | tf_op jit(solution)/shard_map/pallas_call | solution.py:279
  26.7 0.0 collective-permute-done.4.got_one
  26.7 2.3 %collective-permute-done.5.got_two = f32[16,384]{1,0:T(8,128)S(1)} collective-permute-done((f32[16,384]{1,0:T(8,128)S(1)}, f32[16,384]{1,0:T(8,128)S(1)}, u32[]{:S(2)}, u32[]{:S(2)}) %collective-permute-start.5) | collective-permute-done | bytes 24608 | tf_op jit(solution)/shard_map/ppermute | solution.py:298
  29.0 0.0 copy-done.2
  29.0 1.0 %y_kernel.1 = f32[16,16,128]{2,1,0:T(8,128)} custom-call(f32[320,128]{1,0:T(8,128)S(1)} %shard_map.41.main, f32[16,384]{1,0:T(8,128)S(1)} %collective-permute-done.4.got_one, f32[16,384]{1,0:T(8,128)S(1)} %collective-permute-done.5.got_two, f32[16,384]{1,0:T(8,128)S(1)} %get-tuple-element.21.up, f32[16,384]{1,0:T(8,128)S(1)} %get-tuple-element.22.down, ...), custom_call_target="tpu_custom_call" | custom-call | tf_op jit(solution)/shard_map/y_kernel/pallas_call | solution.py:328
  (2 shorter events, 0.0 us)
Async XLA Ops:
  0.0 4.6 %copy-start = (f32[16,16,128]{2,1,0:T(8,128)S(1)}, f32[16,16,128]{2,1,0:T(8,128)}, u32[]{:S(2)}) copy-start(f32[16,16,128]{2,1,0:T(8,128)} %field.3) | copy-start | bytes 393220
  0.0 17.8 %collective-permute-start = (f32[16,16,128]{2,1,0:T(8,128)}, f32[16,16,128]{2,1,0:T(8,128)S(1)}, u32[]{:S(2)}, u32[]{:S(2)}) collective-permute-start(f32[16,16,128]{2,1,0:T(8,128)} %field.3), channel_id=1, source_target_pairs={{64,128},{65,129},{66,130},{67,131},{68,132},{69,133},{70,134},{71... | collective-permute-start | bytes 393224 | tf_op jit(solution)/shard_map/ppermute | solution.py:297
  4.7 13.2 %collective-permute-start.1 = (f32[7,16,128]{2,1,0:T(8,128)S(1)}, f32[7,16,128]{2,1,0:T(8,128)S(1)}, u32[]{:S(2)}, u32[]{:S(2)}) collective-permute-start(f32[7,16,128]{2,1,0:T(8,128)S(1)} %shard_map.38), channel_id=1, source_target_pairs={{0,64},{1,65},{2,66},{3,67},{4,68},{5,69},{6,70},{7,71},{8,72},{9,... | collective-permute-start | bytes 172040 | tf_op jit(solution)/shard_map/ppermute | solution.py:298
  18.0 2.6 %collective-permute-start.2 = (f32[104,128]{1,0:T(8,128)S(1)}, f32[104,128]{1,0:T(8,128)S(1)}, u32[]{:S(2)}, u32[]{:S(2)}) collective-permute-start(f32[104,128]{1,0:T(8,128)S(1)} %get-tuple-element.16), channel_id=1, source_target_pairs={{1,2},{2,1},{3,4},{4,3},{5,6},{6,5},{9,8},{10,9},{11,10},{12,11},{... | collective-permute-start | bytes 159752 | tf_op jit(solution)/shard_map/ppermute | solution.py:297
  18.6 4.9 %collective-permute-start.3 = (f32[104,128]{1,0:T(8,128)S(1)}, f32[104,128]{1,0:T(8,128)S(1)}, u32[]{:S(2)}, u32[]{:S(2)}) collective-permute-start(f32[104,128]{1,0:T(8,128)S(1)} %get-tuple-element.17), channel_id=1, source_target_pairs={{0,1},{1,0},{2,3},{3,2},{4,5},{5,4},{6,7},{7,6},{8,9},{9,10},{10,1... | collective-permute-start | bytes 159752 | tf_op jit(solution)/shard_map/ppermute | solution.py:298
  23.5 2.8 %copy-start.1 = (f32[2,128,128]{2,1,0:T(8,128)S(1)}, f32[2,128,128]{2,1,0:T(8,128)}, u32[]{:S(2)}) copy-start(f32[2,128,128]{2,1,0:T(8,128)} %constant.4.clone.mains) | copy-start | bytes 393220
  23.7 2.9 %collective-permute-start.4 = (f32[16,384]{1,0:T(8,128)S(1)}, f32[16,384]{1,0:T(8,128)S(1)}, u32[]{:S(2)}, u32[]{:S(2)}) collective-permute-start(f32[16,384]{1,0:T(8,128)S(1)} %get-tuple-element.19), channel_id=1, source_target_pairs={{8,16},{9,17},{10,2},{11,3},{12,4},{13,5},{14,6},{15,7},{16,8},{17... | collective-permute-start | bytes 73736 | tf_op jit(solution)/shard_map/ppermute | solution.py:297
  24.4 4.6 %collective-permute-start.5 = (f32[16,384]{1,0:T(8,128)S(1)}, f32[16,384]{1,0:T(8,128)S(1)}, u32[]{:S(2)}, u32[]{:S(2)}) collective-permute-start(f32[16,384]{1,0:T(8,128)S(1)} %get-tuple-element.20), channel_id=1, source_target_pairs={{0,8},{1,9},{2,10},{3,11},{4,12},{5,13},{6,14},{7,15},{8,0},{9,1},... | collective-permute-start | bytes 73736 | tf_op jit(solution)/shard_map/ppermute | solution.py:298
  26.3 2.6 %copy-start.2 = (f32[2,4,16,128]{3,2,1,0:T(8,128)S(1)}, f32[2,4,16,128]{3,2,1,0:T(8,128)}, u32[]{:S(2)}) copy-start(f32[2,4,16,128]{3,2,1,0:T(8,128)} %constant.5.clone.edges) | copy-start | bytes 196612
